TPU v7x, 32 devices: a whole 2x2x4 slice. The times are simulated.
32 devices in a mesh: sa: 2 (over y), gx: 8 (over z, core), gy: 2 (over x).
Axes of the slice: x: 2, y: 2, z: 4, core: 2. Of those that a mesh axis runs over, the one named last changes fastest.
Arguments:
- pred_frames: float32 [12, 4096], P(None, ('sa', 'gx', 'gy')), parts along dimension 1, may hold values from -24 to 24, as said below
- true_frames: float32 [12, 4096], P(None, ('sa', 'gx', 'gy')), parts along dimension 1, may hold values from -24 to 24, as said below
- pred_atoms: float32 [3, 7168], P(None, ('sa', 'gx', 'gy')), parts along dimension 1, may hold values from -24 to 24
- true_atoms: float32 [3, 7168], P(None, ('sa', 'gx', 'gy')), parts along dimension 1, may hold values from -24 to 24
- atom_mask: int32 [7168], P(('sa', 'gx', 'gy')), parts along dimension 0, may hold values from 0 to 1, as said below
- residue_types: int32 [512], P(('sa', 'gx', 'gy')), parts along dimension 0, may hold values from 0 to 19
- swap_flags: int32 [512], P(('sa', 'gx', 'gy')), parts along dimension 0, may hold values from 0 to 1
Outputs:
- frame_loss: float32 [4096], P(('sa', 'gx', 'gy')), parts along dimension 0
- atom_loss: float32 [7168], P(('sa', 'gx', 'gy')), parts along dimension 0
- total_loss: float32 [2], P('sa'), parts along dimension 0
There are 2 independent parts, one for each index of `sa`. A program takes and returns all parts, laid end to end along the dimension named above; each array names one. Nothing has to cross between parts.
Inputs may be any that keep to these rules, and one draw needn't show every extreme that they name: `atom_mask`: atom slots 0 to 3 of every residue, its backbone atoms, are 1. `pred_frames`: rows 0 to 8 of each frame hold a rotation matrix, row-major; rows 9 to 11 its translation. `true_frames`: rows 0 to 8 of each frame hold a rotation matrix, row-major; rows 9 to 11 its translation.
All inputs are finite; a program needn't handle non-finite values.
Results may differ from a plain program's by a relative error of at most 0.0001.
Values sent between devices are 32-bit elements; how exact they have to be, the bound alone decides.
No kernel may reach another device: no remote copies, remote signals or barrier semaphores. Data moves between devices by JAX's collectives and lax.ppermute only.
A program may use at most 64 MiB of HBM per device.

v0:
```python
import math

import jax
import jax.numpy as jnp
import numpy as np
from jax import lax
from jax.sharding import PartitionSpec as P

eps_square = 0.0001
clamp_length = 10.0


def residue_tables():
    atom_counts = np.array([5, 11, 8, 8, 6, 9, 9, 4, 10, 8, 8, 9, 8, 11, 7, 6, 7, 14, 12, 7])
    chi_counts = np.array([0, 4, 2, 2, 1, 3, 3, 0, 2, 2, 2, 4, 3, 2, 2, 1, 1, 2, 2, 1])
    atom_table = (np.arange(14)[None, :] < atom_counts[:, None]).astype(np.float32)
    slot_ids = np.arange(8)[None, :]
    frame_table = (
        (slot_ids == 0) | (slot_ids == 3) | (slot_ids >= 4) & (slot_ids - 3 <= chi_counts[:, None])
    ).astype(np.float32)
    partner_table = np.tile(np.arange(14), (20, 1))
    for restype, swap_pairs in (
        (3, ((6, 7),)),
        (6, ((7, 8),)),
        (13, ((6, 7), (8, 9))),
        (18, ((6, 7), (8, 9))),
    ):
        for first_slot, second_slot in swap_pairs:
            partner_table[restype, first_slot] = second_slot
            partner_table[restype, second_slot] = first_slot
    flip_table = np.zeros((20, 8), np.float32)
    flip_table[3, 5] = 1.0
    flip_table[13, 5] = 1.0
    flip_table[18, 5] = 1.0
    flip_table[6, 6] = 1.0
    sign_table = np.array([1, -1, -1, 1, -1, -1, 1, -1, -1, 1, 1, 1], np.float32)
    return (atom_table, frame_table, partner_table, flip_table, sign_table)


def type_onehot(residue_types):
    return residue_types[:, None] == jnp.arange(20, dtype=jnp.int32)[None, :]


def frame_terms(pred_frames, true_frames, residue_types, swap_flags):
    tables = residue_tables()
    onehot = type_onehot(residue_types).astype(jnp.float32)
    frame_table = jnp.asarray(tables[1], dtype=jnp.float32)
    flip_table = jnp.asarray(tables[3], dtype=jnp.float32)
    sign_table = jnp.asarray(tables[4], dtype=jnp.float32)
    exists = jnp.sum(onehot[:, :, None] * frame_table[None], axis=1)
    flips = jnp.sum(onehot[:, :, None] * flip_table[None], axis=1) * swap_flags[:, None].astype(
        jnp.float32
    )
    residues = residue_types.shape[0]
    shaped = true_frames.reshape(12, residues, 8)
    resolved = jnp.where(flips[None] > 0.5, shaped * sign_table[:, None, None], shaped).reshape(
        12, residues * 8
    )
    rot_pred = pred_frames[:9]
    rot_true = resolved[:9]
    offsets = []
    for column in range(3):
        true_part = (
            rot_true[column] * resolved[9]
            + rot_true[3 + column] * resolved[10]
            + rot_true[6 + column] * resolved[11]
        )
        pred_part = (
            rot_pred[column] * pred_frames[9]
            + rot_pred[3 + column] * pred_frames[10]
            + rot_pred[6 + column] * pred_frames[11]
        )
        offsets.append(true_part - pred_part)
    return (rot_pred, rot_true, jnp.stack(offsets, axis=0), exists.reshape(residues * 8))


def atom_terms(true_atoms, atom_mask, residue_types, swap_flags):
    tables = residue_tables()
    onehot_int = type_onehot(residue_types).astype(jnp.int32)
    onehot = onehot_int.astype(jnp.float32)
    partner_table = jnp.asarray(tables[2], dtype=jnp.int32)
    atom_table = jnp.asarray(tables[0], dtype=jnp.float32)
    partners = jnp.sum(onehot_int[:, :, None] * partner_table[None], axis=1)
    own_slots = jnp.broadcast_to(jnp.arange(14, dtype=jnp.int32)[None, :], partners.shape)
    source = jnp.where(swap_flags[:, None] == 1, partners, own_slots)
    residues = residue_types.shape[0]
    shaped = true_atoms.reshape(3, residues, 14)
    resolved = jnp.take_along_axis(
        shaped, jnp.broadcast_to(source[None], shaped.shape), axis=2
    ).reshape(3, residues * 14)
    mask_resolved = jnp.take_along_axis(atom_mask.reshape(residues, 14), source, axis=1)
    exists = jnp.sum(onehot[:, :, None] * atom_table[None], axis=1)
    weight = (exists * mask_resolved.astype(jnp.float32)).reshape(residues * 14)
    return (resolved, weight)


def clamped_errors(frame_side, atom_side):
    rot_pred, rot_true, offset = frame_side
    pred_pos, true_pos = atom_side
    squares = jnp.zeros((offset.shape[1], pred_pos.shape[1]), jnp.float32)
    for column in range(3):
        error = offset[column][:, None]
        for axis_row in range(3):
            error = error + rot_pred[3 * axis_row + column][:, None] * pred_pos[axis_row][None, :]
            error = error - rot_true[3 * axis_row + column][:, None] * true_pos[axis_row][None, :]
        squares = squares + error * error
    return jnp.minimum(jnp.sqrt(squares + eps_square), clamp_length) / clamp_length


def block_groups(shard_count, shard_cols, pair_limit):
    groups = max(1, min(shard_count, pair_limit // shard_cols))
    while shard_count % groups:
        groups -= 1
    lane_step = 128 // math.gcd(shard_cols, 128)
    return groups


def pair_folder(frame_side, row_exists, shard_cols):
    frame_rows = row_exists.shape[0]
    pair_limit = max(shard_cols, (1 << 20) // frame_rows)

    def add_pairs(carry, pieces, start):
        length = pieces[0].shape[1]
        block_width = length
        shard_count = length // shard_cols
        block_width = block_groups(shard_count, shard_cols, pair_limit) * shard_cols
        turn_count = length // block_width

        def one_block(turn_index, running):
            frame_raw, atom_sum = running
            begin_at = turn_index * block_width
            pred_block = lax.dynamic_slice_in_dim(pieces[0], begin_at, block_width, 1)
            true_block = lax.dynamic_slice_in_dim(pieces[1], begin_at, block_width, 1)
            weight_block = lax.dynamic_slice_in_dim(pieces[2], begin_at, block_width, 1)
            clamped = clamped_errors(frame_side, (pred_block, true_block))
            frame_raw = frame_raw + jnp.sum(clamped * weight_block, axis=1)
            column_sums = jnp.sum(clamped * row_exists[:, None], axis=0)
            atom_sum = lax.dynamic_update_slice_in_dim(atom_sum, column_sums, begin_at, 0)
            return (frame_raw, atom_sum)

        return lax.fori_loop(0, turn_count, one_block, carry)

    return add_pairs


def shards(pred_frames, true_frames, pred_atoms, true_atoms, atom_mask, residue_types, swap_flags):
    rot_pred, rot_true, offset, exists = frame_terms(
        pred_frames, true_frames, residue_types, swap_flags
    )
    true_resolved, weight = atom_terms(true_atoms, atom_mask, residue_types, swap_flags)
    shard_cols = pred_atoms.shape[1]
    rows = (
        lax.all_gather(rot_pred, "gy", axis=1, tiled=True),
        lax.all_gather(rot_true, "gy", axis=1, tiled=True),
        lax.all_gather(offset, "gy", axis=1, tiled=True),
        lax.all_gather(exists[None, :], "gy", axis=1, tiled=True),
    )
    row_exists = rows[3][0]
    folder = pair_folder((rows[0], rows[1], rows[2]), row_exists, shard_cols)
    start_state = (
        jnp.zeros(row_exists.shape, jnp.float32),
        jnp.zeros((shard_cols * lax.axis_size("gx"),), jnp.float32),
    )
    row_raw, column_sum = folder(
        start_state,
        (
            lax.all_gather(pred_atoms, "gx", axis=1, tiled=True),
            lax.all_gather(true_resolved, "gx", axis=1, tiled=True),
            lax.all_gather(weight[None, :], "gx", axis=1, tiled=True),
        ),
        jnp.int32(0),
    )
    frame_raw = lax.psum_scatter(row_raw, "gy", scatter_dimension=0, tiled=True)
    atom_part = lax.psum_scatter(column_sum, "gx", scatter_dimension=0, tiled=True)
    frame_sum = exists * frame_raw
    loss_sum, frame_count, atom_count = lax.psum(
        (jnp.sum(frame_sum), jnp.sum(exists), jnp.sum(weight)), ("gx", "gy")
    )
    frame_loss = frame_sum / atom_count
    atom_loss = weight * atom_part / frame_count
    total_loss = (loss_sum / (frame_count * atom_count)).reshape(1)
    return (frame_loss, atom_loss, total_loss)


def solution(mesh):
    return jax.shard_map(
        shards,
        mesh=mesh,
        in_specs=(
            P(None, ("sa", "gx", "gy")),
            P(None, ("sa", "gx", "gy")),
            P(None, ("sa", "gx", "gy")),
            P(None, ("sa", "gx", "gy")),
            P(("sa", "gx", "gy")),
            P(("sa", "gx", "gy")),
            P(("sa", "gx", "gy")),
        ),
        out_specs=(P(("sa", "gx", "gy")), P(("sa", "gx", "gy")), P("sa")),
        check_vma=False,
    )
```

profile of v0, /device:TPU:0, one launch (start us, length us, event | category | flops | bytes accessed | tf_op | source)
XLA Modules:
  0.0 152.8 jit_solution(3654497878615880032)
XLA Ops:
  0.6 0.7 fusion.10
  1.4 0.8 multiply_reduce_fusion.2
  2.2 0.8 reshape.518
  2.9 1.0 multiply_reduce_fusion.3
  3.9 0.7 broadcast_compare_fusion.2
  4.6 0.1 copy.33
  4.7 0.1 reshape.526
  4.8 1.9 %gather_fusion.1 = s32[224]{0:T(256)S(1)} fusion(s32[16,14]{1,0:T(8,128)S(1)} %reshape.518, s32[224]{0:T(256)S(1)} %reshape.526), kind=kCustom, calls=%fused_computation.1 | custom fusion | bytes 3584 | tf_op jit(solution)/shard_map/jit(take_along_axis)/gather | solution.py:91
  6.9 0.1 copy.34
  7.0 0.6 multiply_reduce_fusion.7
  7.6 0.6 multiply_reduce_fusion.4
  8.4 0.1 reduce_sum.98
  8.5 0.1 broadcast_in_dim.112
  8.7 0.1 reduce_sum.99
  8.9 0.1 broadcast_in_dim.114
  9.0 0.7 fusion.21
  10.4 0.3 dynamic-update-slice
  10.7 5.2 %all_gather.27 = f32[1,256]{1,0:T(1,128)S(1)} all-gather(f32[1,128]{1,0:T(1,128)S(1)} %broadcast_in_dim_reshape.4), channel_id=1, replica_groups=mesh['sa'=2,'gx'=8,'gy'=2] {'gy'}, dimensions={1}, use_global_device_ids=true | all-gather | bytes 1536 | tf_op jit(solution)/shard_map/all_gather | solution.py:156
  15.9 0.1 reshape.516
  16.2 0.1 slice.272
  16.3 4.4 %all_gather.24 = f32[9,256]{1,0:T(8,128)S(1)} all-gather(f32[9,128]{1,0:T(8,128)S(1)} %slice.272), channel_id=1, replica_groups=mesh['sa'=2,'gx'=8,'gy'=2] {'gy'}, dimensions={1}, use_global_device_ids=true | all-gather | bytes 13824 | tf_op jit(solution)/shard_map/all_gather | solution.py:154
  20.7 4.4 %all_gather.22 = f32[9,256]{1,0:T(8,128)S(1)} all-gather(f32[9,128]{1,0:T(8,128)S(1)} %bitcast.65), channel_id=1, replica_groups=mesh['sa'=2,'gx'=8,'gy'=2] {'gy'}, dimensions={1}, use_global_device_ids=true | all-gather | bytes 13824 | tf_op jit(solution)/shard_map/all_gather | solution.py:153
  25.1 0.1 add.253
  25.3 0.1 add.248
  25.4 4.4 %all_gather.21 = f32[3,256]{1,0:T(4,128)S(1)} all-gather(f32[3,128]{1,0:T(4,128)S(1)} %pad_maximum_fusion), channel_id=1, replica_groups=mesh['sa'=2,'gx'=8,'gy'=2] {'gy'}, dimensions={1}, use_global_device_ids=true | all-gather | bytes 4608 | tf_op jit(solution)/shard_map/all_gather | solution.py:155
  30.1 0.1 copy.26
  30.2 0.1 reshape.520
  30.3 9.4 %gather_fusion = f32[672]{0:T(1024)S(1)} fusion(f32[3,16,14]{2,1,0:T(8,128)S(1)} %reshape.517, s32[672]{0:T(1024)S(1)} %reshape.520), kind=kCustom, calls=%fused_computation | custom fusion | bytes 13440 | tf_op jit(solution)/shard_map/jit(take_along_axis)/gather | solution.py:88
  39.8 0.1 broadcast_in_dim.98
  39.9 0.1 reduce_sum.96
  40.1 0.1 broadcast_in_dim.104
  40.3 14.9 %all-gather.1 = f32[8,224,3]{1,2,0:T(4,128)S(1)} all-gather(f32[1,224,3]{1,2,0:T(4,128)S(1)} %select_bitcast_fusion), channel_id=1, replica_groups=mesh['sa'=2,'gx'=8,'gy'=2] {'gx'}, dimensions={0}, use_global_device_ids=true | all-gather | bytes 24192 | tf_op jit(solution)/shard_map/all_gather | solution.py:168
  55.1 0.1 reshape.541
  55.2 14.1 %all-gather = f32[8,224,3]{1,2,0:T(4,128)S(1)} all-gather(f32[1,224,3]{1,2,0:T(4,128)S(1)} %bitcast.66), channel_id=1, replica_groups=mesh['sa'=2,'gx'=8,'gy'=2] {'gx'}, dimensions={0}, use_global_device_ids=true | all-gather | bytes 24192 | tf_op jit(solution)/shard_map/all_gather | solution.py:167
  69.3 0.1 reshape.539
  69.4 0.1 slice_reduce_fusion.4
  69.6 5.2 %multiply_reduce_fusion = f32[1792]{0:T(1024)S(1)} fusion(f32[256]{0:T(256)S(1)} %bitcast.104, f32[256]{0:T(256)S(1)} %bitcast.70, f32[256]{0:T(256)S(1)} %bitcast.88, f32[256]{0:T(256)S(1)} %bitcast.72, f32[256]{0:T(256)S(1)} %bitcast.90, f32[256]{0:T(256)S(1)} %bitcast.74, f32[256]{0:T(256)S(1)} %bitcast.92, f32[256]{0:T(256)S(1)} %bitcast.107, ...), kind=kLoop, calls=%fused_computation.2 | loop fusion | flops 20642048 | bytes 72704 | tf_op jit(solution)/shard_map/while/body/eval_jaxpr/reduce_sum | solution.py:137
  74.7 29.0 %all-reduce.4 = (f32[1792]{0:T(1024)S(1)}, f32[1792]{0:T(1024)S(1)}) all-reduce(f32[1792]{0:T(1024)S(1)} %dynamic-update-slice, f32[1792]{0:T(1024)S(1)} %multiply_reduce_fusion), channel_id=1, replica_groups=mesh['sa'=2,'gx'=8,'gy'=2] {'gx'}, use_global_device_ids=true, to_apply=%add | all-reduce | flops 3584 | bytes 28672
  103.8 3.9 %multiply_reduce_fusion.1 = f32[256]{0:T(256)S(1)} fusion(f32[1792]{0:T(1024)S(1)} %broadcast_multiply_fusion, f32[256]{0:T(256)S(1)} %bitcast.71, f32[256]{0:T(256)S(1)} %bitcast.89, f32[256]{0:T(256)S(1)} %bitcast.73, f32[256]{0:T(256)S(1)} %bitcast.91, f32[256]{0:T(256)S(1)} %bitcast.75, f32[256]{0:T(256)S(1)} %bitcast.93, f32[256]{0:T(256)S(1)} %bitcast.108, ...), kind=kLoop, calls=%fused_computation.3 | loop fusion | flops 20643584 | bytes 72704 | tf_op jit(solution)/shard_map/while/body/eval_jaxpr/reduce_sum | solution.py:136
  107.6 4.9 %all-reduce.1 = f32[256]{0:T(256)S(1)} all-reduce(f32[256]{0:T(256)S(1)} %multiply_reduce_fusion.1), channel_id=2, replica_groups=mesh['sa'=2,'gx'=8,'gy'=2] {'gy'}, use_global_device_ids=true, to_apply=%region_5.6.clone | all-reduce | flops 256 | bytes 2048
  112.6 0.7 dynamic-slice.1
  113.9 0.7 fusion.17
  114.6 31.7 %all-reduce.3 = (f32[]{:T(128)}, f32[]{:T(128)}, f32[]{:T(128)}) all-reduce(f32[]{:T(128)} %multiply_reduce_fusion.7, f32[]{:T(128)} %get-tuple-element.31, f32[]{:T(128)} %fusion.17), channel_id=1, replica_groups=mesh['sa'=2,'gx'=8,'gy'=2] {'gx','gy'}, use_global_device_ids=true, to_apply=%region_7.8 | all-reduce | flops 3 | bytes 24 | tf_op jit(solution)/shard_map/psum | solution.py:176
  146.3 1.2 broadcast_divide_fusion
  148.2 0.1 reduce_sum.103
  148.3 0.1 broadcast_in_dim.119
  148.4 0.1 broadcast_in_dim.121
  148.5 1.3 fusion.16
  (61 shorter events, 1.4 us)
Async XLA Ops:
  4.8 2.8 %copy-start.4 = (f32[20,8]{0,1:T(8,128)S(1)}, f32[20,8]{0,1:T(8,128)}, u32[]{:S(2)}) copy-start(f32[20,8]{0,1:T(8,128)} %constant.66.clone) | copy-start | bytes 1924
  4.8 2.8 %copy-start.5 = (f32[20,8]{0,1:T(8,128)S(1)}, f32[20,8]{0,1:T(8,128)}, u32[]{:S(2)}) copy-start(f32[20,8]{0,1:T(8,128)} %constant.67.clone) | copy-start | bytes 1924
  7.0 2.0 %copy-start.6 = (u32[32]{0:T(128)S(1)}, u32[32]{0:T(128)}, u32[]{:S(2)}) copy-start(u32[32]{0:T(128)} %constant.107) | copy-start | bytes 388
  7.6 8.3 %copy-start.1 = (f32[12,128]{1,0:T(8,128)S(1)}, f32[12,128]{1,0:T(8,128)}, u32[]{:S(2)}) copy-start(f32[12,128]{1,0:T(8,128)} %param.13) | copy-start | bytes 18436
  8.8 7.2 %copy-start.8 = (s32[16]{0:T(128)S(1)}, s32[16]{0:T(128)}, u32[]{:S(2)}) copy-start(s32[16]{0:T(128)} %param.18) | copy-start | bytes 196
  8.9 7.2 %copy-start.7 = (f32[12]{0:T(128)S(1)}, f32[12]{0:T(128)}, u32[]{:S(2)}) copy-start(f32[12]{0:T(128)} %constant.68.clone) | copy-start | bytes 148
  16.2 4.5 %copy-start = (f32[12,128]{1,0:T(8,128)S(1)}, f32[12,128]{1,0:T(8,128)}, u32[]{:S(2)}) copy-start(f32[12,128]{1,0:T(8,128)} %param.12) | copy-start | bytes 18436
  25.1 4.7 %copy-start.2 = (f32[3,224]{1,0:T(4,128)S(1)}, f32[3,224]{1,0:T(4,128)}, u32[]{:S(2)}) copy-start(f32[3,224]{1,0:T(4,128)} %param.15) | copy-start | bytes 8068
  40.1 15.1 %copy-start.3 = (f32[3,224]{1,0:T(4,128)S(1)}, f32[3,224]{1,0:T(4,128)}, u32[]{:S(2)}) copy-start(f32[3,224]{1,0:T(4,128)} %param.14) | copy-start | bytes 8068
  103.8 8.8 %copy-start.9 = (u32[32]{0:T(128)S(1)}, u32[32]{0:T(128)}, u32[]{:S(2)}) copy-start(u32[32]{0:T(128)} %constant.113) | copy-start | bytes 388
where the time goes:
time: 153 us
  blocking collectives  113 us (74%)
  other arithmetic  17 us (11%)
  local copies, waits for them, and re-layouts  16.9 us (11%)
  between operations  6.1 us (4%)
    unnamed x2, blocking collectives  33.9 us
    psum x1, blocking collectives, shards(): lax.psum((jnp.sum(frame_sum), jnp.sum(exists), jnp.sum(weight)), ('gx', '...  31.7 us
    all_gather x1, blocking collectives, shards(): lax.all_gather(true_resolved, 'gx', axis=1, tiled=True)  14.9 us
    all_gather x1, blocking collectives, shards(): lax.all_gather(pred_atoms, 'gx', axis=1, tiled=True)  14.1 us
    gather x3, local copies, waits for them, and re-layouts, atom_terms(): jnp.take_along_axis(shaped, jnp.broadcast_to(source[None], shaped.shape),...  9.56 us
    reduce_sum x1, other arithmetic, one_block(): column_sums = jnp.sum(clamped * row_exists[:, None], axis=0)  5.18 us
    all_gather x1, blocking collectives, shards(): lax.all_gather(exists[None, :], 'gy', axis=1, tiled=True)  5.16 us
    all_gather x1, blocking collectives, shards(): lax.all_gather(offset, 'gy', axis=1, tiled=True)  4.37 us

commit v1 on v0

v1 whole, which is shorter than its diff:
```python
import functools

import jax
import jax.numpy as jnp
import numpy as np
from jax import lax
from jax.experimental import pallas as pl
from jax.experimental.pallas import tpu as pltpu
from jax.sharding import PartitionSpec as P

eps_square = 0.0001
clamp_length = 10.0

ATOM_COUNTS = (5, 11, 8, 8, 6, 9, 9, 4, 10, 8, 8, 9, 8, 11, 7, 6, 7, 14, 12, 7)
CHI_COUNTS = (0, 4, 2, 2, 1, 3, 3, 0, 2, 2, 2, 4, 3, 2, 2, 1, 1, 2, 2, 1)
FRAME_SLOTS = 8
ATOM_SLOTS = 14
WEIGHT_ROW = 6
FRAME_ROWS = 32
EXISTS_ROW = 24
VMEM = pl.BlockSpec(memory_space=pltpu.VMEM)
SMEM = pl.BlockSpec(memory_space=pltpu.SMEM)
PARAMS = pltpu.CompilerParams(vmem_limit_bytes=8 << 20)


def spread_residues(scalars, positions, width):
    value = jnp.full(positions.shape, scalars[0], jnp.int32)
    first = jnp.zeros(positions.shape, jnp.int32)
    for residue in range(1, len(scalars)):
        here = positions >= residue * width
        value = jnp.where(here, scalars[residue], value)
        first = jnp.where(here, residue * width, first)
    return value, positions - first


def table_lookup(types, table):
    value = jnp.full(types.shape, table[0], jnp.int32)
    for kind in range(1, len(table)):
        if table[kind] != table[0]:
            value = jnp.where(types == kind, table[kind], value)
    return value


def prep_kernel(types_ref, flags_ref, pf_ref, tf_ref, pa_ref, ta_ref, mask_ref, atoms_ref, frames_ref, pad_ref):
    residues = types_ref.shape[0]
    copies, _, lanes = atoms_ref.shape
    frames = pf_ref.shape[1]
    own_atoms = pa_ref.shape[1]
    codes = [types_ref[r] + 32 * flags_ref[r] for r in range(residues)]

    place = lax.broadcasted_iota(jnp.int32, (1, frames), 1)
    code, slot = spread_residues(codes, place, FRAME_SLOTS)
    types = code & 31
    swapped = code >= 32
    chi = table_lookup(types, CHI_COUNTS)
    exists = (slot == 0) | (slot == 3) | ((slot >= 4) & (slot - 3 <= chi))
    half_turn = ((types == 3) | (types == 13) | (types == 18)) & (slot == 5)
    half_turn = swapped & (half_turn | ((types == 6) & (slot == 6)))
    sign = jnp.where(half_turn, -1.0, 1.0)
    rot_pred = [[pf_ref[pl.ds(3 * a + c, 1), :] for c in range(3)] for a in range(3)]
    rot_true = [[tf_ref[pl.ds(3 * a + c, 1), :] for c in range(3)] for a in range(3)]
    rot_true = [[row[0], row[1] * sign, row[2] * sign] for row in rot_true]
    zero = jnp.zeros((1, frames), jnp.float32)
    one = jnp.ones((1, frames), jnp.float32)
    rows = []
    for a in range(3):
        rel = []
        for b in range(3):
            rel.append(
                rot_pred[a][0] * rot_true[b][0]
                + rot_pred[a][1] * rot_true[b][1]
                + rot_pred[a][2] * rot_true[b][2]
            )
        shift = rel[0] * tf_ref[9:10, :] + rel[1] * tf_ref[10:11, :] + rel[2] * tf_ref[11:12, :]
        shift = shift - pf_ref[pl.ds(9 + a, 1), :]
        rows += [one if a == k else zero for k in range(3)]
        rows += [-rel[0], -rel[1], -rel[2], zero, shift]
    for index, row in enumerate(rows):
        frames_ref[pl.ds(index, 1), :] = row
    frames_ref[pl.ds(EXISTS_ROW, 8), :] = jnp.zeros((8, frames), jnp.float32)
    frames_ref[pl.ds(EXISTS_ROW, 1), :] = jnp.where(exists, 1.0, 0.0)

    pad_ref[...] = jnp.zeros(pad_ref.shape, jnp.float32)
    pad_ref[0:3, 0:own_atoms] = pa_ref[...]
    pad_ref[3:6, 0:own_atoms] = ta_ref[...]
    pad_ref[6:7, 0:own_atoms] = mask_ref[...].astype(jnp.float32)
    block = pad_ref[...]
    place = lax.broadcasted_iota(jnp.int32, (1, lanes), 1)
    code, slot = spread_residues(codes, place, ATOM_SLOTS)
    types = code & 31
    swapped = code >= 32
    twice = (types == 13) | (types == 18)

    def opens_pair(s):
        pair = ((s == 6) & ((types == 3) | twice)) | ((s == 7) & (types == 6)) | ((s == 8) & twice)
        return swapped & pair

    after = jnp.where(opens_pair(slot), 1, 0)
    before = jnp.where(opens_pair(slot - 1), 1, 0)
    row = lax.broadcasted_iota(jnp.int32, (8, lanes), 0)
    renamed = jnp.where(
        jnp.broadcast_to(after, (8, lanes)) == 1,
        pltpu.roll(block, lanes - 1, 1),
        jnp.where(jnp.broadcast_to(before, (8, lanes)) == 1, pltpu.roll(block, 1, 1), block),
    )
    block = jnp.where(row < 3, block, renamed)
    real = (slot < table_lookup(types, ATOM_COUNTS)) & (place < own_atoms)
    real = jnp.broadcast_to(jnp.where(real, 1, 0), (8, lanes)) == 1
    block = jnp.where((row == WEIGHT_ROW) & ~real, 0.0, block)
    block = jnp.where(row == 7, 1.0, block)
    for copy in range(copies):
        atoms_ref[copy] = block


def split_rows(x):
    high = x.astype(jnp.bfloat16).astype(jnp.float32)
    rest = x - high
    middle = rest.astype(jnp.bfloat16).astype(jnp.float32)
    return high, middle, rest - middle


def pair_kernel(axes, *refs):
    gx, gy = axes
    atoms_ref = refs[0]
    frame_refs = refs[1 : 1 + gy]
    out_ref = refs[1 + gy]
    lhs_ref, exist_ref, row_ref = refs[2 + gy :]
    frames = frame_refs[0].shape[1]
    lanes = atoms_ref.shape[2]
    chunk = 64
    my_gx = lax.axis_index("gx")
    my_gy = lax.axis_index("gy")

    for block, ref in enumerate(frame_refs):
        for c in range(3):
            high, middle, low = split_rows(ref[pl.ds(8 * c, 8), :])
            zeros = jnp.zeros((frames - 48, frames), jnp.float32)
            stacked = jnp.concatenate([high, middle, low, high, middle, high, zeros], axis=0)
            lhs_ref[c, pl.ds(block * frames, frames), :] = stacked.T.astype(jnp.bfloat16)
        wide = jnp.broadcast_to(ref[pl.ds(EXISTS_ROW, 1), :] * clamp_length, (frames, frames))
        exist_ref[pl.ds(block * frames, frames), :] = wide.T
    row_ref[...] = jnp.zeros(row_ref.shape, jnp.float32)
    out_ref[...] = jnp.zeros(out_ref.shape, jnp.float32)

    def one_source(source, carry):
        block = atoms_ref[source]
        high, middle, low = split_rows(block)
        rhs = jnp.concatenate([high, high, high, middle, middle, low], axis=0).astype(jnp.bfloat16)
        cap = block[WEIGHT_ROW : WEIGHT_ROW + 1] * clamp_length
        column = jnp.zeros((8, lanes), jnp.float32)
        for start in range(0, gy * frames, chunk):
            square = eps_square
            for c in range(3):
                w = jnp.dot(
                    lhs_ref[c, pl.ds(start, chunk), pl.ds(0, 48)], rhs, preferred_element_type=jnp.float32
                )
                square = square + w * w
            limit = exist_ref[pl.ds(start, chunk), :]
            distance = square * lax.rsqrt(square)
            distance = jnp.minimum(jnp.minimum(distance, cap), jnp.concatenate([limit] * (lanes // 128), axis=1))
            total = row_ref[pl.ds(start, chunk), :]
            for lane in range(0, lanes, 128):
                total = total + distance[:, lane : lane + 128]
            row_ref[pl.ds(start, chunk), :] = total
            column = column + jnp.sum(distance.reshape(chunk // 8, 8, lanes), axis=0)
        sums = jnp.sum(column, axis=0, keepdims=True)
        slot = source * gy + my_gy
        for lane in range(0, lanes, 128):
            out_ref[slot, pl.ds(lane // 128, 1), :] = sums[:, lane : lane + 128]
        return carry

    lax.fori_loop(0, gx, one_source, 0)

    loss = jnp.zeros((1, 128), jnp.float32)
    for block in range(gy):
        sums = jnp.sum(row_ref[pl.ds(block * frames, frames), :].T, axis=0, keepdims=True)
        owner = lax.rem(my_gy + block, gy)
        out_ref[my_gx * gy + owner, pl.ds(lanes // 128, 1), :] = sums
        loss = loss + sums
    lane = lax.broadcasted_iota(jnp.int32, (1, 128), 1)
    loss = jnp.sum(loss, axis=1, keepdims=True)
    frame_count = jnp.sum(frame_refs[0][pl.ds(EXISTS_ROW, 1), :], axis=1, keepdims=True)
    atom_count = jnp.sum(atoms_ref[my_gx][WEIGHT_ROW : WEIGHT_ROW + 1], axis=1, keepdims=True)
    scalars = jnp.where(lane == 0, loss, jnp.where(lane == 1, frame_count, atom_count))
    for slot in range(gx * gy):
        out_ref[slot, pl.ds(lanes // 128 + 1, 1), :] = scalars


def finish_kernel(parts_ref, frame_ref, atom_ref, total_ref):
    sums = parts_ref[0]
    for slot in range(1, parts_ref.shape[0]):
        sums = sums + parts_ref[slot]
    atom_rows = sums.shape[0] - 2
    scalars = sums[atom_rows + 1 : atom_rows + 2]
    loss = scalars[:, 0:1]
    frame_count = scalars[:, 1:2]
    atom_count = scalars[:, 2:3]
    scale = 1.0 / clamp_length
    frame_ref[...] = sums[atom_rows : atom_rows + 1] * scale / atom_count
    atoms = jnp.concatenate([sums[i : i + 1] for i in range(atom_rows)], axis=1) * scale / frame_count
    atom_ref[...] = atoms[:, : atom_ref.shape[1]]
    total_ref[...] = loss * scale / (frame_count * atom_count)


def shards(pred_frames, true_frames, pred_atoms, true_atoms, atom_mask, residue_types, swap_flags):
    gx = lax.axis_size("gx")
    gy = lax.axis_size("gy")
    frames = pred_frames.shape[1]
    own_atoms = pred_atoms.shape[1]
    lanes = -(-own_atoms // 128) * 128
    rows = lanes // 128 + 2
    f32 = jnp.float32
    atoms, own_frames = pl.pallas_call(
        prep_kernel,
        out_shape=(
            jax.ShapeDtypeStruct((gx, 8, lanes), f32),
            jax.ShapeDtypeStruct((FRAME_ROWS, frames), f32),
        ),
        in_specs=[SMEM, SMEM, VMEM, VMEM, VMEM, VMEM, VMEM],
        out_specs=(VMEM, VMEM),
        scratch_shapes=[pltpu.VMEM((8, lanes), f32)],
        compiler_params=PARAMS,
        name="prep",
    )(residue_types, swap_flags, pred_frames, true_frames, pred_atoms, true_atoms, atom_mask.reshape(1, own_atoms))
    frame_blocks = [own_frames]
    for step in range(1, gy):
        pairs = [((i + step) % gy, i) for i in range(gy)]
        frame_blocks.append(lax.ppermute(own_frames, "gy", pairs))
    atoms = lax.all_to_all(atoms, "gx", 0, 0, tiled=True)
    parts = pl.pallas_call(
        functools.partial(pair_kernel, (gx, gy)),
        out_shape=jax.ShapeDtypeStruct((gx * gy, rows, 128), f32),
        in_specs=[VMEM] * (1 + gy),
        out_specs=VMEM,
        scratch_shapes=[
            pltpu.VMEM((3, gy * frames, 128), jnp.bfloat16),
            pltpu.VMEM((gy * frames, 128), f32),
            pltpu.VMEM((gy * frames, 128), f32),
        ],
        compiler_params=PARAMS,
        name="pairs",
    )(atoms, *frame_blocks)
    parts = lax.all_to_all(parts, ("gx", "gy"), 0, 0, tiled=True)
    frame_loss, atom_loss, total_loss = pl.pallas_call(
        finish_kernel,
        out_shape=(
            jax.ShapeDtypeStruct((1, frames), f32),
            jax.ShapeDtypeStruct((1, own_atoms), f32),
            jax.ShapeDtypeStruct((1, 1), f32),
        ),
        in_specs=[VMEM],
        out_specs=(VMEM, VMEM, VMEM),
        compiler_params=PARAMS,
        name="finish",
    )(parts)
    return (frame_loss.reshape(frames), atom_loss.reshape(own_atoms), total_loss.reshape(1))


def solution(mesh):
    both = P(None, ("sa", "gx", "gy"))
    flat = P(("sa", "gx", "gy"))
    return jax.shard_map(
        shards,
        mesh=mesh,
        in_specs=(both, both, both, both, flat, flat, flat),
        out_specs=(flat, flat, P("sa")),
        check_vma=False,
    )
```

time: 153 us -> 32.2 us (0.21)
  blocking collectives: 113 us -> 10.3 us
  other arithmetic: 17 us -> 0 us
  local copies, waits for them, and re-layouts: 16.9 us -> 4.1 us
  starting transfers between devices: 0 us -> 7.84 us
  between operations: 6.1 us -> 0.66 us
  Pallas kernels: 0 us -> 4.45 us
  waiting for transfers between devices: 0 us -> 4.43 us
    all_gather x6 -> x0, blocking collectives: 47.2 us -> none  [the longest x1 14.9 us: shards(): lax.all_gather(true_resolved, 'gx', axis=1, tiled=True)]
    unnamed x2 -> x0, blocking collectives: 33.9 us -> none
    psum x1 -> x0, blocking collectives: 31.7 us -> none  [shards(): lax.psum((jnp.sum(frame_sum), jnp.sum(exists), jnp.sum(weight)), ('gx', '...]
    reduce_sum x7 -> x0, other arithmetic: 12.8 us -> none  [the longest x1 5.18 us: one_block(): column_sums = jnp.sum(clamped * row_exists[:, None], axis=0)]
    gather x8 -> x0, local copies, waits for them, and re-layouts: 11.8 us -> none  [the longest x3 9.56 us: atom_terms(): jnp.take_along_axis(shaped, jnp.broadcast_to(source[None], shaped.shape),...]
    all_to_all x0 -> x1, blocking collectives: none -> 10.3 us  [shards(): parts = lax.all_to_all(parts, ('gx', 'gy'), 0, 0, tiled=True)]
    all_to_all x0 -> x1, starting transfers between devices: none -> 6.35 us  [shards(): atoms = lax.all_to_all(atoms, 'gx', 0, 0, tiled=True)]
    pallas_call x0 -> x3, Pallas kernels: none -> 4.45 us  [the longest x1 2.53 us: shards(): pl.pallas_call(functools.partial(pair_kernel, (gx, gy)), out_shape=jax.Sh...]
  transfers between devices with their start and end apart: 0 -> 2, of which waited for: 0 -> 2; matrix products, arithmetic and copies ran while one was open for 0% -> 0% of each run, Pallas kernels for 0% -> 0%
where the time goes in v1:
time: 32.2 us; the launch traced here: 31.7 us
  blocking collectives  10.3 us (32%)
  starting transfers between devices  7.84 us (24%)
  Pallas kernels  4.45 us (14%)
  waiting for transfers between devices  4.43 us (14%)
  local copies, waits for them, and re-layouts  4.1 us (13%)
  between operations  0.66 us (2%)
    all_to_all x1, blocking collectives, shards(): parts = lax.all_to_all(parts, ('gx', 'gy'), 0, 0, tiled=True)  10.3 us
    all_to_all x1, starting transfers between devices, shards(): atoms = lax.all_to_all(atoms, 'gx', 0, 0, tiled=True)  6.35 us
    unnamed x14, local copies, waits for them, and re-layouts  4.1 us
    pallas_call x1, Pallas kernels, shards(): pl.pallas_call(functools.partial(pair_kernel, (gx, gy)), out_shape=jax.Sh...  2.53 us
    ppermute x1, waiting for transfers between devices, shards(): frame_blocks.append(lax.ppermute(own_frames, 'gy', pairs))  2.25 us
    all_to_all x1, waiting for transfers between devices, shards(): atoms = lax.all_to_all(atoms, 'gx', 0, 0, tiled=True)  2.18 us
    ppermute x1, starting transfers between devices, shards(): frame_blocks.append(lax.ppermute(own_frames, 'gy', pairs))  1.49 us
    pallas_call x1, Pallas kernels, shards(): pl.pallas_call(prep_kernel, out_shape=(jax.ShapeDtypeStruct((gx, 8, lanes...  1.25 us
  transfers between devices with their start and end apart: 2, of which 2 were waited for; matrix products, arithmetic and copies ran while one was open for 0% of the time, Pallas kernels for 0%

profile of v1, /device:TPU:0, one launch (start us, length us, event | category | flops | bytes accessed | tf_op | source)
XLA Modules:
  0.0 31.7 jit_solution(18017750974233816565)
XLA Ops:
  0.6 0.0 copy-start.5
  0.6 0.0 copy-start.4
  0.7 0.6 %copy-done.5 = s32[16]{0:T(128)S(1)} copy-done((s32[16]{0:T(128)S(1)}, s32[16]{0:T(128)}, u32[]{:S(2)}) %copy-start.5) | copy-done | bytes 88
  1.3 0.0 copy-done.4
  1.3 0.0 copy-start
  1.3 0.7 %copy-done = f32[12,128]{1,0:T(8,128)S(1)} copy-done((f32[12,128]{1,0:T(8,128)S(1)}, f32[12,128]{1,0:T(8,128)}, u32[]{:S(2)}) %copy-start) | copy-done | bytes 6168
  2.0 0.0 copy-start.1
  2.0 0.7 %copy-done.1 = f32[12,128]{1,0:T(8,128)S(1)} copy-done((f32[12,128]{1,0:T(8,128)S(1)}, f32[12,128]{1,0:T(8,128)}, u32[]{:S(2)}) %copy-start.1) | copy-done | bytes 6168
  2.7 0.0 copy-start.2
  2.7 0.7 %copy-done.2 = f32[3,224]{1,0:T(4,128)S(1)} copy-done((f32[3,224]{1,0:T(4,128)S(1)}, f32[3,224]{1,0:T(4,128)}, u32[]{:S(2)}) %copy-start.2) | copy-done | bytes 2712
  3.4 0.0 copy-start.3
  3.4 0.7 %copy-done.3 = f32[3,224]{1,0:T(4,128)S(1)} copy-done((f32[3,224]{1,0:T(4,128)S(1)}, f32[3,224]{1,0:T(4,128)}, u32[]{:S(2)}) %copy-start.3) | copy-done | bytes 2712
  4.1 0.0 copy-start.6
  4.1 0.7 %copy-done.6 = s32[16]{0:T(128)S(1)} copy-done((s32[16]{0:T(128)S(1)}, s32[16]{0:T(128)}, u32[]{:S(2)}) %copy-start.6) | copy-done | bytes 88
  4.8 1.2 %prep.1 = (f32[8,8,256]{2,1,0:T(8,128)}, f32[32,128]{1,0:T(8,128)S(1)}) custom-call(s32[16]{0:T(128)S(1)} %copy-done.5, s32[16]{0:T(128)S(1)} %copy-done.6, f32[12,128]{1,0:T(8,128)S(1)} %copy-done, f32[12,128]{1,0:T(8,128)S(1)} %copy-done.1, f32[3,224]{1,0:T(4,128)S(1)} %copy-done.2, f32[3,224]{1,0:T(4,128)S(1)} %copy-done.3, s32[1,224]{1,0:T(1,128)S(1)} %bitcast.4), custom_call_target="tpu_custom_call" | custom-call | tf_op jit(solution)/shard_map/prep/pallas_call | solution.py:213
  6.0 6.4 %all-to-all-start = ((f32[8,8,256]{2,1,0:T(8,128)}), f32[8,8,256]{2,1,0:T(8,128)S(1)}, u32[]{:S(2)}, u32[]{:S(2)}) async-start(f32[8,8,256]{2,1,0:T(8,128)} %get-tuple-element.8), calls=%async_computation | async-start | bytes 131072 | tf_op jit(solution)/shard_map/all_to_all | solution.py:229
  12.4 1.5 %collective-permute-start = (f32[32,128]{1,0:T(8,128)S(1)}, f32[32,128]{1,0:T(8,128)S(1)}, u32[]{:S(2)}, u32[]{:S(2)}) collective-permute-start(f32[32,128]{1,0:T(8,128)S(1)} %get-tuple-element.9.refs_1_), channel_id=1, source_target_pairs={{1,0},{0,1},{3,2},{2,3},{5,4},{4,5},{7,6},{6,7},{9,8},{8,9},{11,10... | collective-permute-start | bytes 49160 | tf_op jit(solution)/shard_map/ppermute | solution.py:228
  13.8 2.2 %collective-permute-done.refs_2_ = f32[32,128]{1,0:T(8,128)S(1)} collective-permute-done((f32[32,128]{1,0:T(8,128)S(1)}, f32[32,128]{1,0:T(8,128)S(1)}, u32[]{:S(2)}, u32[]{:S(2)}) %collective-permute-start) | collective-permute-done | bytes 16416 | tf_op jit(solution)/shard_map/ppermute | solution.py:228
  16.1 2.2 %all-to-all-done.refs_0_ = f32[8,8,256]{2,1,0:T(8,128)S(1)} async-done(((f32[8,8,256]{2,1,0:T(8,128)}), f32[8,8,256]{2,1,0:T(8,128)S(1)}, u32[]{:S(2)}, u32[]{:S(2)}) %all-to-all-start) | async-done | bytes 65568 | tf_op jit(solution)/shard_map/all_to_all | solution.py:229
  18.3 2.5 %pairs.1 = f32[16,4,128]{2,1,0:T(4,128)S(1)} custom-call(f32[8,8,256]{2,1,0:T(8,128)S(1)} %all-to-all-done.refs_0_, f32[32,128]{1,0:T(8,128)S(1)} %get-tuple-element.9.refs_1_, f32[32,128]{1,0:T(8,128)S(1)} %collective-permute-done.refs_2_), custom_call_target="tpu_custom_call" | custom-call | tf_op jit(solution)/shard_map/pairs/pallas_call | solution.py:230
  20.8 10.3 %all_to_all.10.parts_ref = f32[16,4,128]{2,1,0:T(4,128)S(1)} all-to-all(f32[16,4,128]{2,1,0:T(4,128)S(1)} %pairs.1), channel_id=1, replica_groups=mesh['sa'=2,'gx'=8,'gy'=2] {'gx','gy'}, dimensions={0} | all-to-all | bytes 65536 | tf_op jit(solution)/shard_map/all_to_all | solution.py:243
  31.1 0.7 %finish.1 = (f32[1,128]{1,0:T(1,128)}, f32[1,224]{1,0:T(1,128)}, f32[1,1]{1,0:T(1,128)}) custom-call(f32[16,4,128]{2,1,0:T(4,128)S(1)} %all_to_all.10.parts_ref), custom_call_target="tpu_custom_call" | custom-call | tf_op jit(solution)/shard_map/finish/pallas_call | solution.py:244
Async XLA Ops:
  0.6 0.7 %copy-start.5 = (s32[16]{0:T(128)S(1)}, s32[16]{0:T(128)}, u32[]{:S(2)}) copy-start(s32[16]{0:T(128)} %types_ref.1) | copy-start | bytes 196
  0.6 0.7 %copy-start.4 = (s32[224]{0:T(256)S(1)}, s32[224]{0:T(256)}, u32[]{:S(2)}) copy-start(s32[224]{0:T(256)} %param.11) | copy-start | bytes 2692
  1.3 0.7 %copy-start = (f32[12,128]{1,0:T(8,128)S(1)}, f32[12,128]{1,0:T(8,128)}, u32[]{:S(2)}) copy-start(f32[12,128]{1,0:T(8,128)} %pf_ref.1) | copy-start | bytes 18436
  2.0 0.7 %copy-start.1 = (f32[12,128]{1,0:T(8,128)S(1)}, f32[12,128]{1,0:T(8,128)}, u32[]{:S(2)}) copy-start(f32[12,128]{1,0:T(8,128)} %tf_ref.1) | copy-start | bytes 18436
  2.7 0.7 %copy-start.2 = (f32[3,224]{1,0:T(4,128)S(1)}, f32[3,224]{1,0:T(4,128)}, u32[]{:S(2)}) copy-start(f32[3,224]{1,0:T(4,128)} %pa_ref.1) | copy-start | bytes 8068
  3.4 0.7 %copy-start.3 = (f32[3,224]{1,0:T(4,128)S(1)}, f32[3,224]{1,0:T(4,128)}, u32[]{:S(2)}) copy-start(f32[3,224]{1,0:T(4,128)} %ta_ref.1) | copy-start | bytes 8068
  4.1 0.7 %copy-start.6 = (s32[16]{0:T(128)S(1)}, s32[16]{0:T(128)}, u32[]{:S(2)}) copy-start(s32[16]{0:T(128)} %flags_ref.1) | copy-start | bytes 196
  6.0 12.3 %all-to-all-start = ((f32[8,8,256]{2,1,0:T(8,128)}), f32[8,8,256]{2,1,0:T(8,128)S(1)}, u32[]{:S(2)}, u32[]{:S(2)}) async-start(f32[8,8,256]{2,1,0:T(8,128)} %get-tuple-element.8), calls=%async_computation | async-start | bytes 131072 | tf_op jit(solution)/shard_map/all_to_all | solution.py:229
  12.4 3.7 %collective-permute-start = (f32[32,128]{1,0:T(8,128)S(1)}, f32[32,128]{1,0:T(8,128)S(1)}, u32[]{:S(2)}, u32[]{:S(2)}) collective-permute-start(f32[32,128]{1,0:T(8,128)S(1)} %get-tuple-element.9.refs_1_), channel_id=1, source_target_pairs={{1,0},{0,1},{3,2},{2,3},{5,4},{4,5},{7,6},{6,7},{9,8},{8,9},{11,10... | collective-permute-start | bytes 49160 | tf_op jit(solution)/shard_map/ppermute | solution.py:228

commit v2 on v1

--- a/solution.py
+++ b/solution.py
@@ -2,7 +2,6 @@
 
 import jax
 import jax.numpy as jnp
-import numpy as np
 from jax import lax
 from jax.experimental import pallas as pl
 from jax.experimental.pallas import tpu as pltpu
@@ -19,7 +18,7 @@
 FRAME_ROWS = 32
 EXISTS_ROW = 24
 VMEM = pl.BlockSpec(memory_space=pltpu.VMEM)
-SMEM = pl.BlockSpec(memory_space=pltpu.SMEM)
+HBM = pl.BlockSpec(memory_space=pltpu.HBM)
 PARAMS = pltpu.CompilerParams(vmem_limit_bytes=8 << 20)
 
 
@@ -41,7 +40,14 @@
     return value
 
 
-def prep_kernel(types_ref, flags_ref, pf_ref, tf_ref, pa_ref, ta_ref, mask_ref, atoms_ref, frames_ref, pad_ref):
+def prep_kernel(*refs):
+    inputs, (atoms_ref, frames_ref), scratch = refs[:7], refs[7:9], refs[9:]
+    (types_ref, flags_ref, pf_ref, tf_ref, pa_ref, ta_ref, mask_ref, pad_ref, sems) = scratch
+    fetches = [pltpu.make_async_copy(src, dst, sems.at[i]) for i, (src, dst) in enumerate(zip(inputs, scratch))]
+    for fetch in fetches:
+        fetch.start()
+    for fetch in fetches:
+        fetch.wait()
     residues = types_ref.shape[0]
     copies, _, lanes = atoms_ref.shape
     frames = pf_ref.shape[1]
@@ -210,18 +216,30 @@
     lanes = -(-own_atoms // 128) * 128
     rows = lanes // 128 + 2
     f32 = jnp.float32
+    inputs = (residue_types, swap_flags, pred_frames, true_frames, pred_atoms, true_atoms)
+    inputs += (atom_mask.reshape(1, own_atoms),)
     atoms, own_frames = pl.pallas_call(
         prep_kernel,
         out_shape=(
             jax.ShapeDtypeStruct((gx, 8, lanes), f32),
             jax.ShapeDtypeStruct((FRAME_ROWS, frames), f32),
         ),
-        in_specs=[SMEM, SMEM, VMEM, VMEM, VMEM, VMEM, VMEM],
+        in_specs=[HBM] * 7,
         out_specs=(VMEM, VMEM),
-        scratch_shapes=[pltpu.VMEM((8, lanes), f32)],
+        scratch_shapes=[
+            pltpu.SMEM(residue_types.shape, jnp.int32),
+            pltpu.SMEM(swap_flags.shape, jnp.int32),
+            pltpu.VMEM(pred_frames.shape, f32),
+            pltpu.VMEM(true_frames.shape, f32),
+            pltpu.VMEM(pred_atoms.shape, f32),
+            pltpu.VMEM(true_atoms.shape, f32),
+            pltpu.VMEM((1, own_atoms), jnp.int32),
+            pltpu.VMEM((8, lanes), f32),
+            pltpu.SemaphoreType.DMA((7,)),
+        ],
         compiler_params=PARAMS,
         name="prep",
-    )(residue_types, swap_flags, pred_frames, true_frames, pred_atoms, true_atoms, atom_mask.reshape(1, own_atoms))
+    )(*[pltpu.with_memory_space_constraint(x, pltpu.HBM) for x in inputs])
     frame_blocks = [own_frames]
     for step in range(1, gy):
         pairs = [((i + step) % gy, i) for i in range(gy)]

time: 32.2 us -> 28.2 us (0.88)
  local copies, waits for them, and re-layouts: 4.1 us -> 0 us
    unnamed x14 -> x0, local copies, waits for them, and re-layouts: 4.1 us -> none
where the time goes in v2:
time: 28.2 us; the launch traced here: 27.9 us
  blocking collectives  10.3 us (37%)
  starting transfers between devices  7.86 us (28%)
  Pallas kernels  4.7 us (17%)
  waiting for transfers between devices  4.43 us (16%)
  between operations  0.64 us (2%)
    all_to_all x1, blocking collectives, shards(): parts = lax.all_to_all(parts, ('gx', 'gy'), 0, 0, tiled=True)  10.3 us
    all_to_all x1, starting transfers between devices, shards(): atoms = lax.all_to_all(atoms, 'gx', 0, 0, tiled=True)  6.37 us
    pallas_call x1, Pallas kernels, shards(): pl.pallas_call(functools.partial(pair_kernel, (gx, gy)), out_shape=jax.Sh...  2.52 us
    ppermute x1, waiting for transfers between devices, shards(): frame_blocks.append(lax.ppermute(own_frames, 'gy', pairs))  2.25 us
    all_to_all x1, waiting for transfers between devices, shards(): atoms = lax.all_to_all(atoms, 'gx', 0, 0, tiled=True)  2.18 us
    pallas_call x1, Pallas kernels, shards(): pl.pallas_call(prep_kernel, out_shape=(jax.ShapeDtypeStruct((gx, 8, lanes...  1.51 us
    ppermute x1, starting transfers between devices, shards(): frame_blocks.append(lax.ppermute(own_frames, 'gy', pairs))  1.49 us
    pallas_call x1, Pallas kernels, shards(): pl.pallas_call(finish_kernel, out_shape=(jax.ShapeDtypeStruct((1, frames)...  0.67 us
  transfers between devices with their start and end apart: 2, of which 2 were waited for; matrix products, arithmetic and copies ran while one was open for 0% of the time, Pallas kernels for 0%

profile of v2, /device:TPU:0, one launch (start us, length us, event | category | flops | bytes accessed | tf_op | source)
XLA Modules:
  0.0 27.9 jit_solution(12710953493339301906)
XLA Ops:
  0.6 1.5 %prep.1 = (f32[8,8,256]{2,1,0:T(8,128)}, f32[32,128]{1,0:T(8,128)S(1)}) custom-call(s32[16]{0:T(128)} %refs_0_.1, s32[16]{0:T(128)} %refs_1_.1, f32[12,128]{1,0:T(8,128)} %refs_2_.1, f32[12,128]{1,0:T(8,128)} %refs_3_.1, f32[3,224]{1,0:T(4,128)} %refs_4_.1, f32[3,224]{1,0:T(4,128)} %refs_5_.1, s32[1,224]{1,0:T(1,128)} %bitcast.4), custom_call_target="tpu_custom_call" | custom-call | tf_op jit(solution)/shard_map/prep/pallas_call | solution.py:221
  2.2 6.4 %all-to-all-start = ((f32[8,8,256]{2,1,0:T(8,128)}), f32[8,8,256]{2,1,0:T(8,128)S(1)}, u32[]{:S(2)}, u32[]{:S(2)}) async-start(f32[8,8,256]{2,1,0:T(8,128)} %get-tuple-element.8), calls=%async_computation | async-start | bytes 131072 | tf_op jit(solution)/shard_map/all_to_all | solution.py:247
  8.5 1.5 %collective-permute-start = (f32[32,128]{1,0:T(8,128)S(1)}, f32[32,128]{1,0:T(8,128)S(1)}, u32[]{:S(2)}, u32[]{:S(2)}) collective-permute-start(f32[32,128]{1,0:T(8,128)S(1)} %get-tuple-element.9.refs_1_), channel_id=1, source_target_pairs={{1,0},{0,1},{3,2},{2,3},{5,4},{4,5},{7,6},{6,7},{9,8},{8,9},{11,10... | collective-permute-start | bytes 49160 | tf_op jit(solution)/shard_map/ppermute | solution.py:246
  10.0 2.2 %collective-permute-done.refs_2_ = f32[32,128]{1,0:T(8,128)S(1)} collective-permute-done((f32[32,128]{1,0:T(8,128)S(1)}, f32[32,128]{1,0:T(8,128)S(1)}, u32[]{:S(2)}, u32[]{:S(2)}) %collective-permute-start) | collective-permute-done | bytes 16416 | tf_op jit(solution)/shard_map/ppermute | solution.py:246
  12.3 2.2 %all-to-all-done.refs_0_ = f32[8,8,256]{2,1,0:T(8,128)S(1)} async-done(((f32[8,8,256]{2,1,0:T(8,128)}), f32[8,8,256]{2,1,0:T(8,128)S(1)}, u32[]{:S(2)}, u32[]{:S(2)}) %all-to-all-start) | async-done | bytes 65568 | tf_op jit(solution)/shard_map/all_to_all | solution.py:247
  14.4 2.5 %pairs.1 = f32[16,4,128]{2,1,0:T(4,128)S(1)} custom-call(f32[8,8,256]{2,1,0:T(8,128)S(1)} %all-to-all-done.refs_0_, f32[32,128]{1,0:T(8,128)S(1)} %get-tuple-element.9.refs_1_, f32[32,128]{1,0:T(8,128)S(1)} %collective-permute-done.refs_2_), custom_call_target="tpu_custom_call" | custom-call | tf_op jit(solution)/shard_map/pairs/pallas_call | solution.py:248
  17.0 10.3 %all_to_all.10.parts_ref = f32[16,4,128]{2,1,0:T(4,128)S(1)} all-to-all(f32[16,4,128]{2,1,0:T(4,128)S(1)} %pairs.1), channel_id=1, replica_groups=mesh['sa'=2,'gx'=8,'gy'=2] {'gx','gy'}, dimensions={0} | all-to-all | bytes 65536 | tf_op jit(solution)/shard_map/all_to_all | solution.py:261
  27.2 0.7 %finish.1 = (f32[1,128]{1,0:T(1,128)}, f32[1,224]{1,0:T(1,128)}, f32[1,1]{1,0:T(1,128)}) custom-call(f32[16,4,128]{2,1,0:T(4,128)S(1)} %all_to_all.10.parts_ref), custom_call_target="tpu_custom_call" | custom-call | tf_op jit(solution)/shard_map/finish/pallas_call | solution.py:262
Async XLA Ops:
  2.2 12.3 %all-to-all-start = ((f32[8,8,256]{2,1,0:T(8,128)}), f32[8,8,256]{2,1,0:T(8,128)S(1)}, u32[]{:S(2)}, u32[]{:S(2)}) async-start(f32[8,8,256]{2,1,0:T(8,128)} %get-tuple-element.8), calls=%async_computation | async-start | bytes 131072 | tf_op jit(solution)/shard_map/all_to_all | solution.py:247
  8.5 3.7 %collective-permute-start = (f32[32,128]{1,0:T(8,128)S(1)}, f32[32,128]{1,0:T(8,128)S(1)}, u32[]{:S(2)}, u32[]{:S(2)}) collective-permute-start(f32[32,128]{1,0:T(8,128)S(1)} %get-tuple-element.9.refs_1_), channel_id=1, source_target_pairs={{1,0},{0,1},{3,2},{2,3},{5,4},{4,5},{7,6},{6,7},{9,8},{8,9},{11,10... | collective-permute-start | bytes 49160 | tf_op jit(solution)/shard_map/ppermute | solution.py:246

commit v3 on v2

v3 whole, which is shorter than its diff:
```python
import functools

import jax
import jax.numpy as jnp
from jax import lax
from jax.experimental import pallas as pl
from jax.experimental.pallas import tpu as pltpu
from jax.sharding import PartitionSpec as P

eps_square = 0.0001
clamp_length = 10.0

ATOM_COUNTS = (5, 11, 8, 8, 6, 9, 9, 4, 10, 8, 8, 9, 8, 11, 7, 6, 7, 14, 12, 7)
CHI_COUNTS = (0, 4, 2, 2, 1, 3, 3, 0, 2, 2, 2, 4, 3, 2, 2, 1, 1, 2, 2, 1)
FRAME_SLOTS = 8
USED_SLOTS = 6
ATOM_SLOTS = 14
ROW_CHUNK = 384
TILE = 256
TILE_GROUP = 2
VMEM = pl.BlockSpec(memory_space=pltpu.VMEM)
HBM = pl.BlockSpec(memory_space=pltpu.HBM)


def spread_residues(scalars, positions, width):
    value = jnp.full(positions.shape, scalars[0], jnp.int32)
    first = jnp.zeros(positions.shape, jnp.int32)
    for residue in range(1, len(scalars)):
        here = positions >= residue * width
        value = jnp.where(here, scalars[residue], value)
        first = jnp.where(here, residue * width, first)
    return value, positions - first


def table_lookup(types, table):
    value = jnp.full(types.shape, table[0], jnp.int32)
    for kind in range(1, len(table)):
        if table[kind] != table[0]:
            value = jnp.where(types == kind, table[kind], value)
    return value


def split_rows(x):
    high = x.astype(jnp.bfloat16).astype(jnp.float32)
    rest = x - high
    middle = rest.astype(jnp.bfloat16).astype(jnp.float32)
    return high, middle, rest - middle


def one_hot(rank):
    size = rank.shape[1]
    place = lax.broadcasted_iota(jnp.int32, (size, size), 0)
    return jnp.where(place == rank, 1.0, 0.0).astype(jnp.bfloat16)


def exact_dot(x, selection, contract):
    rows = x.shape[0]
    parts = jnp.concatenate(split_rows(x), axis=0).astype(jnp.bfloat16)
    out = lax.dot_general(parts, selection, (((1,), (contract,)), ((), ())), preferred_element_type=jnp.float32)
    return out[:rows] + out[rows : 2 * rows] + out[2 * rows :]


def prep_kernel(*refs):
    inputs, (block_ref, rank_ref), scratch = refs[:7], refs[7:9], refs[9:]
    (types_ref, flags_ref, pf_ref, tf_ref, pa_ref, ta_ref, mask_ref, pad_ref, sems) = scratch
    fetches = [pltpu.make_async_copy(src, dst, sems.at[i]) for i, (src, dst) in enumerate(zip(inputs, scratch))]
    for fetch in fetches:
        fetch.start()
    residues = types_ref.shape[0]
    frames = pf_ref.shape[1]
    own_atoms = pa_ref.shape[1]
    lanes = pad_ref.shape[1]
    pad_ref[...] = jnp.zeros(pad_ref.shape, jnp.float32)
    for fetch in fetches:
        fetch.wait()
    codes = [types_ref[r] + 32 * flags_ref[r] for r in range(residues)]

    pad_ref[0:3, 0:own_atoms] = pa_ref[...]
    pad_ref[3:6, 0:own_atoms] = ta_ref[...]
    pad_ref[6:7, 0:own_atoms] = mask_ref[...].astype(jnp.float32)
    atoms = pad_ref[...]
    place = lax.broadcasted_iota(jnp.int32, (1, lanes), 1)
    code, slot = spread_residues(codes, place, ATOM_SLOTS)
    types = code & 31
    swapped = code >= 32
    twice = (types == 13) | (types == 18)

    def opens_pair(s):
        pair = ((s == 6) & ((types == 3) | twice)) | ((s == 7) & (types == 6)) | ((s == 8) & twice)
        return swapped & pair

    after = jnp.where(opens_pair(slot), 1, 0)
    before = jnp.where(opens_pair(slot - 1), 1, 0)
    row = lax.broadcasted_iota(jnp.int32, (8, lanes), 0)
    renamed = jnp.where(
        jnp.broadcast_to(after, (8, lanes)) == 1,
        pltpu.roll(atoms, lanes - 1, 1),
        jnp.where(jnp.broadcast_to(before, (8, lanes)) == 1, pltpu.roll(atoms, 1, 1), atoms),
    )
    atoms = jnp.where(row < 3, atoms, renamed)
    real = (slot < table_lookup(types, ATOM_COUNTS)) & (place < own_atoms)
    real = jnp.broadcast_to(jnp.where(real, 1, 0), (8, lanes)) == 1
    atoms = jnp.where((row == 6) & ~real, 0.0, atoms)
    weight = atoms[6:7]
    earlier = lax.broadcasted_iota(jnp.int32, (lanes, lanes), 0) < lax.broadcasted_iota(jnp.int32, (lanes, lanes), 1)
    earlier = jnp.where(earlier, 1.0, 0.0).astype(jnp.bfloat16)
    rank = jnp.dot(
        jnp.broadcast_to(weight, (16, lanes)).astype(jnp.bfloat16), earlier, preferred_element_type=jnp.float32
    )[0:1]
    atom_rank = jnp.where(weight > 0.5, rank, -1.0).astype(jnp.int32)
    atom_count = jnp.sum(weight, axis=1, keepdims=True)

    place = lax.broadcasted_iota(jnp.int32, (1, frames), 1)
    code, slot = spread_residues(codes, place, FRAME_SLOTS)
    types = code & 31
    swapped = code >= 32
    chi = table_lookup(types, CHI_COUNTS)
    exists = (slot == 0) | (slot == 3) | ((slot >= 4) & (slot - 3 <= chi))
    exists = jnp.where(exists, 1.0, 0.0)
    half_turn = ((types == 3) | (types == 13) | (types == 18)) & (slot == 5)
    half_turn = swapped & (half_turn | ((types == 6) & (slot == 6)))
    sign = jnp.where(half_turn, -1.0, 1.0)
    rot_pred = [[pf_ref[pl.ds(3 * a + c, 1), :] for c in range(3)] for a in range(3)]
    rot_true = [[tf_ref[pl.ds(3 * a + c, 1), :] for c in range(3)] for a in range(3)]
    rot_true = [[r[0], r[1] * sign, r[2] * sign] for r in rot_true]
    rows = []
    shifts = []
    for a in range(3):
        rel = [
            rot_pred[a][0] * rot_true[b][0] + rot_pred[a][1] * rot_true[b][1] + rot_pred[a][2] * rot_true[b][2]
            for b in range(3)
        ]
        shift = rel[0] * tf_ref[9:10, :] + rel[1] * tf_ref[10:11, :] + rel[2] * tf_ref[11:12, :]
        shifts.append(shift - pf_ref[pl.ds(9 + a, 1), :])
        if a < 2:
            rows += [-rel[0], -rel[1], -rel[2]]
    rows += shifts + [exists]
    rows += [jnp.zeros((16 - len(rows), frames), jnp.float32)]
    rank = jnp.dot(
        jnp.broadcast_to(exists, (16, frames)).astype(jnp.bfloat16),
        earlier[:frames, :frames],
        preferred_element_type=jnp.float32,
    )[0:1]
    frame_rank = jnp.where(exists > 0.5, rank, -1.0).astype(jnp.int32)
    frame_count = jnp.sum(exists, axis=1, keepdims=True)

    atoms = exact_dot(atoms, one_hot(atom_rank), 1)
    packed = exact_dot(jnp.concatenate(rows, axis=0), one_hot(frame_rank), 1)
    first = jnp.where(place == 0, frame_count, jnp.where(place == 1, atom_count, packed[9:10]))
    extra = jnp.concatenate([first, packed[8:9]], axis=1)
    atoms = jnp.where(row == 7, jnp.broadcast_to(extra, (8, lanes)), atoms)
    block = jnp.concatenate([atoms, packed[0:8]], axis=1)
    for copy in range(block_ref.shape[0]):
        block_ref[copy] = block
    rank_ref[...] = jnp.zeros(rank_ref.shape, jnp.int32)
    rank_ref[0:1, :] = atom_rank
    rank_ref[1:2, 0:frames] = frame_rank


def pair_kernel(
    gy_size, blocks_ref, rank_ref, frame_ref, atom_ref, total_ref, src_ref, rhs_ref, lhs_ref, row_ref, col_ref
):
    devices = blocks_ref.shape[0]
    frames = frame_ref.shape[1]
    own_atoms = atom_ref.shape[1]
    most = frames * USED_SLOTS // FRAME_SLOTS // 16
    row_step = ROW_CHUNK // 16
    per_tile = TILE // 128
    me = lax.axis_index("gx") * gy_size + lax.axis_index("gy")
    lane = lax.broadcasted_iota(jnp.int32, (8, 128), 1)
    sub = lax.broadcasted_iota(jnp.int32, (8, 128), 0)
    src_ref[...] = jnp.zeros(src_ref.shape, jnp.float32)
    col_ref[...] = jnp.zeros(col_ref.shape, jnp.float32)

    def place_block(device, carry):
        atoms_before, rows_before, frame_total, my_atoms, my_rows = carry
        my_atoms = jnp.where(device == me, atoms_before, my_atoms)
        my_rows = jnp.where(device == me, rows_before, my_rows)
        frame_count = jnp.max(blocks_ref[device, 7:8, 0:1]).astype(jnp.int32)
        atom_count = jnp.max(blocks_ref[device, 7:8, 1:2]).astype(jnp.int32)
        tile = atoms_before // 128
        turn = atoms_before % 128
        low = pltpu.roll(blocks_ref[device, :, 0:128], turn, 1)
        high = pltpu.roll(blocks_ref[device, :, 128:256], turn, 1)
        inside = lane >= turn
        src_ref[tile] += jnp.where(inside, low, 0.0)
        src_ref[tile + 1] += jnp.where(inside, high, low)
        src_ref[tile + 2] += jnp.where(inside, 0.0, high)
        part = blocks_ref[device, :, 256:384]
        exists = blocks_ref[device, 7:8, 0:128]
        exists = jnp.where(lane[0:1] < 2, 1.0, exists)
        last = blocks_ref[device, 7:8, 128:256]
        a = [part[k : k + 1] for k in range(3)]
        b = [part[3 + k : 4 + k] for k in range(3)]
        cross = [a[2] * b[1] - a[1] * b[2], a[0] * b[2] - a[2] * b[0], a[1] * b[0] - a[0] * b[1]]
        rotations = (part[0:3], part[3:6], jnp.concatenate(cross, axis=0))
        shifts = (part[6:7], part[7:8], last)
        for c in range(3):
            group = jnp.concatenate([rotations[c], rotations[c], shifts[c], exists], axis=0)
            high, middle, low = split_rows(group)
            ones = jnp.broadcast_to(exists, (8, 128))
            stack = [
                jnp.where((sub >= 3) & (sub < 6), middle, high),
                jnp.where(sub < 3, low, jnp.where(sub == 6, middle, high)),
                jnp.where(sub < 3, middle, jnp.where(sub == 6, low, high)),
            ]
            stack = [x if k == c else jnp.where(sub == 7, 0.0, x) for k, x in enumerate(stack)]
            stack.append(jnp.where((sub == c) | (sub == 3 + c), ones, 0.0))
            stack.append(jnp.zeros((96, 128), jnp.float32))
            turned = jnp.concatenate(stack, axis=0).T[: 16 * most]
            lhs_ref[pl.ds(rows_before, most), c] = turned.astype(jnp.bfloat16).reshape(most, 16, 128)
        return (
            atoms_before + atom_count,
            rows_before + (frame_count + 15) // 16,
            frame_total + frame_count,
            my_atoms,
            my_rows,
        )

    group = 16
    while devices % group:
        group //= 2

    def place_group(index, carry):
        for k in range(group):
            carry = place_block(index * group + k, carry)
        return carry

    carry = (0, 0, 0, 0, 0)
    if devices == group:
        carry = place_group(0, carry)
    else:
        carry = lax.fori_loop(0, devices // group, place_group, carry)
    atom_total, row_total, frame_total, my_atoms, my_rows = carry
    lhs_ref[pl.ds(row_total, row_step)] = jnp.zeros((row_step,) + lhs_ref.shape[1:], jnp.bfloat16)
    chunks = (row_total + row_step - 1) // row_step
    behind = pl.multiple_of(chunks * ROW_CHUNK, ROW_CHUNK)
    row_ref[pl.ds(behind, frames), :] = jnp.zeros((frames, 128), jnp.float32)
    width = TILE * TILE_GROUP
    groups = (atom_total + width - 1) // width

    def build_rhs(index, carry):
        for k in range(TILE_GROUP):
            tile = index * TILE_GROUP + k
            x = jnp.concatenate([src_ref[tile * per_tile + m] for m in range(per_tile)], axis=1)
            high, middle, low = split_rows(x)
            one = jnp.ones((1, TILE), jnp.float32)
            nil = jnp.zeros((2, TILE), jnp.float32)
            rows = [high[3:6], high[3:6], one, high[0:1], high[3:6], middle[3:6], one, high[1:2]]
            rows += [middle[3:6], low[3:6], one, high[2:3], middle[0:3], low[0:3], nil]
            rhs_ref[tile] = jnp.concatenate(rows, axis=0).astype(jnp.bfloat16)
        return carry

    lax.fori_loop(0, groups, build_rhs, 0)

    def one_chunk(chunk, carry):
        start = pl.multiple_of(chunk * ROW_CHUNK, ROW_CHUNK)
        row_ref[pl.ds(start, ROW_CHUNK), :] = jnp.zeros((ROW_CHUNK, 128), jnp.float32)

        def one_group(index, carry):
            lhs = lhs_ref[pl.ds(chunk * row_step, row_step)].reshape(3 * ROW_CHUNK, 128)[:, 0:32]
            row_sums = [None] * (ROW_CHUNK // 8)
            for k in range(TILE_GROUP):
                tile = index * TILE_GROUP + k
                w = jnp.dot(lhs, rhs_ref[tile], preferred_element_type=jnp.float32)
                cap = jnp.concatenate([src_ref[tile * per_tile + m, 6:7, :] for m in range(per_tile)], axis=1)
                cap = jnp.broadcast_to(cap * clamp_length, (8, TILE))
                column = None
                for g in range(ROW_CHUNK // 8):
                    base = 48 * (g // 2) + 8 * (g % 2)
                    w0, w1, w2 = (w[base + 16 * c : base + 16 * c + 8] for c in range(3))
                    square = (w0 * w0 + w1 * w1) + (w2 * w2 + eps_square)
                    distance = jnp.minimum(square * lax.rsqrt(square), cap)
                    column = distance if column is None else column + distance
                    for m in range(per_tile):
                        piece = distance[:, 128 * m : 128 * m + 128]
                        row_sums[g] = piece if row_sums[g] is None else row_sums[g] + piece
                for m in range(per_tile):
                    col_ref[tile * per_tile + m] += column[:, 128 * m : 128 * m + 128]
            for g in range(ROW_CHUNK // 8):
                row_ref[pl.ds(start + 8 * g, 8), :] += row_sums[g]
            return carry

        return lax.fori_loop(0, groups, one_group, carry)

    lax.fori_loop(0, chunks, one_chunk, 0)

    idle = (chunks * ROW_CHUNK - frame_total).astype(jnp.float32)
    least = jnp.full((1, 128), eps_square, jnp.float32)
    least = least * lax.rsqrt(least)

    def column_sums(tile):
        cap = src_ref[tile, 6:7, :] * clamp_length
        return jnp.sum(col_ref[tile], axis=0, keepdims=True) - idle * jnp.minimum(least, cap)

    def add_tile(tile, carry):
        sums, floor = carry
        return sums + col_ref[tile], floor + jnp.minimum(least, src_ref[tile, 6:7, :] * clamp_length)

    sums, floor = lax.fori_loop(
        0,
        groups * per_tile * TILE_GROUP,
        add_tile,
        (jnp.zeros((8, 128), jnp.float32), jnp.zeros((1, 128), jnp.float32)),
    )
    loss = jnp.sum(sums, axis=0, keepdims=True) - idle * floor
    loss = jnp.sum(loss, axis=1, keepdims=True)
    atom_number = atom_total.astype(jnp.float32)
    frame_number = frame_total.astype(jnp.float32)
    scale = 1.0 / clamp_length
    total_ref[...] = loss * scale / (frame_number * atom_number)

    tile = my_atoms // 128
    turn = my_atoms % 128
    back = (128 - turn) % 128
    pieces = [pltpu.roll(jnp.broadcast_to(column_sums(tile + k), (8, 128)), back, 1) for k in range(3)]
    keep = lane < 128 - turn
    mine = jnp.concatenate([jnp.where(keep, pieces[k], pieces[k + 1]) for k in range(2)], axis=1)
    mine = exact_dot(mine, one_hot(rank_ref[0:1, :]), 0)[0:1]
    atom_ref[...] = mine[:, :own_atoms] * scale / frame_number

    rows = row_ref[pl.ds(pl.multiple_of(my_rows * 16, 16), frames), :]
    mine = jnp.broadcast_to(jnp.sum(rows.T, axis=0, keepdims=True), (8, frames))
    mine = exact_dot(mine, one_hot(rank_ref[1:2, 0:frames]), 0)[0:1]
    frame_ref[...] = mine * scale / atom_number


def shards(pred_frames, true_frames, pred_atoms, true_atoms, atom_mask, residue_types, swap_flags):
    devices = lax.axis_size("gx") * lax.axis_size("gy")
    frames = pred_frames.shape[1]
    own_atoms = pred_atoms.shape[1]
    lanes = -(-own_atoms // 128) * 128
    f32 = jnp.float32
    inputs = (residue_types, swap_flags, pred_frames, true_frames, pred_atoms, true_atoms)
    inputs += (atom_mask.reshape(1, own_atoms),)
    blocks, ranks = pl.pallas_call(
        prep_kernel,
        out_shape=(
            jax.ShapeDtypeStruct((devices, 8, lanes + frames), f32),
            jax.ShapeDtypeStruct((8, lanes), jnp.int32),
        ),
        in_specs=[HBM] * 7,
        out_specs=(VMEM, VMEM),
        scratch_shapes=[
            pltpu.SMEM(residue_types.shape, jnp.int32),
            pltpu.SMEM(swap_flags.shape, jnp.int32),
            pltpu.VMEM(pred_frames.shape, f32),
            pltpu.VMEM(true_frames.shape, f32),
            pltpu.VMEM(pred_atoms.shape, f32),
            pltpu.VMEM(true_atoms.shape, f32),
            pltpu.VMEM((1, own_atoms), jnp.int32),
            pltpu.VMEM((8, lanes), f32),
            pltpu.SemaphoreType.DMA((7,)),
        ],
        compiler_params=pltpu.CompilerParams(vmem_limit_bytes=8 << 20),
        name="prep",
    )(*[pltpu.with_memory_space_constraint(x, pltpu.HBM) for x in inputs])
    blocks = lax.all_to_all(blocks, ("gx", "gy"), 0, 0, tiled=True)
    width = TILE * TILE_GROUP
    groups = -(-(devices * own_atoms + 256) // width)
    row_groups = devices * (frames * USED_SLOTS // FRAME_SLOTS // 16) + 2 * ROW_CHUNK // 16
    scratch = [
        ((groups * width // 128, 8, 128), f32),
        ((groups * TILE_GROUP, 32, TILE), jnp.bfloat16),
        ((row_groups, 3, 16, 128), jnp.bfloat16),
        ((row_groups * 16, 128), f32),
        ((groups * width // 128, 8, 128), f32),
    ]
    room = sum(jnp.dtype(dtype).itemsize * functools.reduce(lambda a, b: a * b, shape) for shape, dtype in scratch)
    frame_loss, atom_loss, total_loss = pl.pallas_call(
        functools.partial(pair_kernel, lax.axis_size("gy")),
        out_shape=(
            jax.ShapeDtypeStruct((1, frames), f32),
            jax.ShapeDtypeStruct((1, own_atoms), f32),
            jax.ShapeDtypeStruct((1, 1), f32),
        ),
        in_specs=[VMEM, VMEM],
        out_specs=(VMEM, VMEM, VMEM),
        scratch_shapes=[pltpu.VMEM(shape, dtype) for shape, dtype in scratch],
        compiler_params=pltpu.CompilerParams(vmem_limit_bytes=room + (12 << 20)),
        name="pairs",
    )(blocks, ranks)
    return (frame_loss.reshape(frames), atom_loss.reshape(own_atoms), total_loss.reshape(1))


def solution(mesh):
    both = P(None, ("sa", "gx", "gy"))
    flat = P(("sa", "gx", "gy"))
    return jax.shard_map(
        shards,
        mesh=mesh,
        in_specs=(both, both, both, both, flat, flat, flat),
        out_specs=(flat, flat, P("sa")),
        check_vma=False,
    )
```

time: 28.2 us -> 25.7 us (0.911)
  starting transfers between devices: 7.86 us -> 0 us
  blocking collectives: 10.3 us -> 15.9 us
  waiting for transfers between devices: 4.43 us -> 0 us
  Pallas kernels: 4.7 us -> 8.94 us
    all_to_all x1 -> x0, starting transfers between devices: 6.37 us -> none  [shards(): atoms = lax.all_to_all(atoms, 'gx', 0, 0, tiled=True)]
    all_to_all x1, blocking collectives: 10.3 us -> 15.9 us  [shards(): blocks = lax.all_to_all(blocks, ('gx', 'gy'), 0, 0, tiled=True)]
    pallas_call x3 -> x2, Pallas kernels: 4.7 us -> 8.94 us  [the longest x1 7.73 us: shards(): pl.pallas_call(functools.partial(pair_kernel, lax.axis_size('gy')), out_s...]
    ppermute x1 -> x0, waiting for transfers between devices: 2.25 us -> none  [shards(): frame_blocks.append(lax.ppermute(own_frames, 'gy', pairs))]
    all_to_all x1 -> x0, waiting for transfers between devices: 2.18 us -> none  [shards(): atoms = lax.all_to_all(atoms, 'gx', 0, 0, tiled=True)]
    ppermute x1 -> x0, starting transfers between devices: 1.49 us -> none  [shards(): frame_blocks.append(lax.ppermute(own_frames, 'gy', pairs))]
  transfers between devices with their start and end apart: 2 -> 0, of which waited for: 2 -> 0; matrix products, arithmetic and copies ran while one was open for 0% -> 0% of each run, Pallas kernels for 0% -> 0%
where the time goes in v3:
time: 25.7 us; the launch traced here: 25.5 us
  blocking collectives  15.9 us (62%)
  Pallas kernels  8.94 us (35%)
  between operations  0.64 us (2%)
    all_to_all x1, blocking collectives, shards(): blocks = lax.all_to_all(blocks, ('gx', 'gy'), 0, 0, tiled=True)  15.9 us
    pallas_call x1, Pallas kernels, shards(): pl.pallas_call(functools.partial(pair_kernel, lax.axis_size('gy')), out_s...  7.73 us
    pallas_call x1, Pallas kernels, shards(): pl.pallas_call(prep_kernel, out_shape=(jax.ShapeDtypeStruct((devices, 8,...  1.21 us

profile of v3, /device:TPU:0, one launch (start us, length us, event | category | flops | bytes accessed | tf_op | source)
XLA Modules:
  0.0 25.5 jit_solution(17480591067916313505)
XLA Ops:
  0.6 1.2 %prep.1 = (f32[16,8,384]{2,1,0:T(8,128)S(1)}, s32[8,256]{1,0:T(8,128)S(1)}) custom-call(s32[16]{0:T(128)} %refs_0_.1, s32[16]{0:T(128)} %refs_1_.1, f32[12,128]{1,0:T(8,128)} %refs_2_.1, f32[12,128]{1,0:T(8,128)} %refs_3_.1, f32[3,224]{1,0:T(4,128)} %refs_4_.1, f32[3,224]{1,0:T(4,128)} %refs_5_.1, s32[1,224]{1,0:T(1,128)} %bitcast.4), custom_call_target="tpu_custom_call" | custom-call | tf_op jit(solution)/shard_map/prep/pallas_call | solution.py:336
  1.8 15.9 %all_to_all.5.blocks_ref = f32[16,8,384]{2,1,0:T(8,128)S(1)} all-to-all(f32[16,8,384]{2,1,0:T(8,128)S(1)} %get-tuple-element.8), channel_id=1, replica_groups=mesh['sa'=2,'gx'=8,'gy'=2] {'gx','gy'}, dimensions={0} | all-to-all | bytes 393216 | tf_op jit(solution)/shard_map/all_to_all | solution.py:358
  17.7 7.7 %pairs.1 = (f32[1,128]{1,0:T(1,128)}, f32[1,224]{1,0:T(1,128)}, f32[1,1]{1,0:T(1,128)}) custom-call(f32[16,8,384]{2,1,0:T(8,128)S(1)} %all_to_all.5.blocks_ref, s32[8,256]{1,0:T(8,128)S(1)} %get-tuple-element.9.rank_ref), custom_call_target="tpu_custom_call" | custom-call | tf_op jit(solution)/shard_map/pairs/pallas_call | solution.py:370

commit v4 on v3

--- a/solution.py
+++ b/solution.py
@@ -14,10 +14,11 @@
 CHI_COUNTS = (0, 4, 2, 2, 1, 3, 3, 0, 2, 2, 2, 4, 3, 2, 2, 1, 1, 2, 2, 1)
 FRAME_SLOTS = 8
 USED_SLOTS = 6
+BUILD_GROUP = 4
 ATOM_SLOTS = 14
-ROW_CHUNK = 384
+ROW_CHUNK = 352
 TILE = 256
-TILE_GROUP = 2
+TILE_GROUP = 4
 VMEM = pl.BlockSpec(memory_space=pltpu.VMEM)
 HBM = pl.BlockSpec(memory_space=pltpu.HBM)
 
@@ -150,72 +151,67 @@
     extra = jnp.concatenate([first, packed[8:9]], axis=1)
     atoms = jnp.where(row == 7, jnp.broadcast_to(extra, (8, lanes)), atoms)
     block = jnp.concatenate([atoms, packed[0:8]], axis=1)
-    for copy in range(block_ref.shape[0]):
-        block_ref[copy] = block
+    block_ref[0] = block
     rank_ref[...] = jnp.zeros(rank_ref.shape, jnp.int32)
     rank_ref[0:1, :] = atom_rank
     rank_ref[1:2, 0:frames] = frame_rank
 
 
+def exchange_steps(gx_size, gy_size):
+    steps = [("gy", 1 << k) for k in range(gy_size.bit_length() - 1)]
+    steps += [("gx", 1 << k) for k in range(1, gx_size.bit_length() - 1)]
+    return steps + [("gx", 1)]
+
+
+def device_code(gx_size, gy_size):
+    code = 0
+    for k, (axis, step) in enumerate(exchange_steps(gx_size, gy_size)):
+        code = code + jnp.where(lax.axis_index(axis) & step != 0, 1 << k, 0)
+    return code
+
+
 def pair_kernel(
-    gy_size, blocks_ref, rank_ref, frame_ref, atom_ref, total_ref, src_ref, rhs_ref, lhs_ref, row_ref, col_ref
+    sizes, blocks_ref, rank_ref, frame_ref, atom_ref, total_ref, src_ref, fsrc_ref, rhs_ref, lhs_ref, row_ref, col_ref
 ):
     devices = blocks_ref.shape[0]
     frames = frame_ref.shape[1]
     own_atoms = atom_ref.shape[1]
-    most = frames * USED_SLOTS // FRAME_SLOTS // 16
     row_step = ROW_CHUNK // 16
     per_tile = TILE // 128
-    me = lax.axis_index("gx") * gy_size + lax.axis_index("gy")
+    me = device_code(*sizes)
     lane = lax.broadcasted_iota(jnp.int32, (8, 128), 1)
     sub = lax.broadcasted_iota(jnp.int32, (8, 128), 0)
     src_ref[...] = jnp.zeros(src_ref.shape, jnp.float32)
+    fsrc_ref[...] = jnp.zeros(fsrc_ref.shape, jnp.float32)
     col_ref[...] = jnp.zeros(col_ref.shape, jnp.float32)
 
     def place_block(device, carry):
-        atoms_before, rows_before, frame_total, my_atoms, my_rows = carry
+        atoms_before, frames_before, my_atoms, my_frames = carry
         my_atoms = jnp.where(device == me, atoms_before, my_atoms)
-        my_rows = jnp.where(device == me, rows_before, my_rows)
-        frame_count = jnp.max(blocks_ref[device, 7:8, 0:1]).astype(jnp.int32)
-        atom_count = jnp.max(blocks_ref[device, 7:8, 1:2]).astype(jnp.int32)
+        my_frames = jnp.where(device == me, frames_before, my_frames)
+        block = jnp.bitwise_xor(me, device)
+        frame_count = jnp.max(blocks_ref[block, 7:8, 0:1]).astype(jnp.int32)
+        atom_count = jnp.max(blocks_ref[block, 7:8, 1:2]).astype(jnp.int32)
         tile = atoms_before // 128
         turn = atoms_before % 128
-        low = pltpu.roll(blocks_ref[device, :, 0:128], turn, 1)
-        high = pltpu.roll(blocks_ref[device, :, 128:256], turn, 1)
+        low = pltpu.roll(blocks_ref[block, :, 0:128], turn, 1)
+        high = pltpu.roll(blocks_ref[block, :, 128:256], turn, 1)
         inside = lane >= turn
         src_ref[tile] += jnp.where(inside, low, 0.0)
         src_ref[tile + 1] += jnp.where(inside, high, low)
         src_ref[tile + 2] += jnp.where(inside, 0.0, high)
-        part = blocks_ref[device, :, 256:384]
-        exists = blocks_ref[device, 7:8, 0:128]
-        exists = jnp.where(lane[0:1] < 2, 1.0, exists)
-        last = blocks_ref[device, 7:8, 128:256]
-        a = [part[k : k + 1] for k in range(3)]
-        b = [part[3 + k : 4 + k] for k in range(3)]
-        cross = [a[2] * b[1] - a[1] * b[2], a[0] * b[2] - a[2] * b[0], a[1] * b[0] - a[0] * b[1]]
-        rotations = (part[0:3], part[3:6], jnp.concatenate(cross, axis=0))
-        shifts = (part[6:7], part[7:8], last)
-        for c in range(3):
-            group = jnp.concatenate([rotations[c], rotations[c], shifts[c], exists], axis=0)
-            high, middle, low = split_rows(group)
-            ones = jnp.broadcast_to(exists, (8, 128))
-            stack = [
-                jnp.where((sub >= 3) & (sub < 6), middle, high),
-                jnp.where(sub < 3, low, jnp.where(sub == 6, middle, high)),
-                jnp.where(sub < 3, middle, jnp.where(sub == 6, low, high)),
-            ]
-            stack = [x if k == c else jnp.where(sub == 7, 0.0, x) for k, x in enumerate(stack)]
-            stack.append(jnp.where((sub == c) | (sub == 3 + c), ones, 0.0))
-            stack.append(jnp.zeros((96, 128), jnp.float32))
-            turned = jnp.concatenate(stack, axis=0).T[: 16 * most]
-            lhs_ref[pl.ds(rows_before, most), c] = turned.astype(jnp.bfloat16).reshape(most, 16, 128)
-        return (
-            atoms_before + atom_count,
-            rows_before + (frame_count + 15) // 16,
-            frame_total + frame_count,
-            my_atoms,
-            my_rows,
-        )
+        exists = jnp.where(lane[0:1] < 2, 1.0, blocks_ref[block, 7:8, 0:128])
+        last = jnp.broadcast_to(blocks_ref[block, 7:8, 128:256], (8, 128))
+        tile = frames_before // 128
+        turn = frames_before % 128
+        low = pltpu.roll(blocks_ref[block, :, 256:384], turn, 1)
+        high = pltpu.roll(jnp.where(sub == 0, last, jnp.broadcast_to(exists, (8, 128))), turn, 1)
+        inside = lane >= turn
+        fsrc_ref[tile, 0:8] += jnp.where(inside, low, 0.0)
+        fsrc_ref[tile, 8:16] += jnp.where(inside, high, 0.0)
+        fsrc_ref[tile + 1, 0:8] += jnp.where(inside, 0.0, low)
+        fsrc_ref[tile + 1, 8:16] += jnp.where(inside, 0.0, high)
+        return (atoms_before + atom_count, frames_before + frame_count, my_atoms, my_frames)
 
     group = 16
     while devices % group:
@@ -226,18 +222,48 @@
             carry = place_block(index * group + k, carry)
         return carry
 
-    carry = (0, 0, 0, 0, 0)
+    carry = (0, 0, 0, 0)
     if devices == group:
         carry = place_group(0, carry)
     else:
         carry = lax.fori_loop(0, devices // group, place_group, carry)
-    atom_total, row_total, frame_total, my_atoms, my_rows = carry
-    lhs_ref[pl.ds(row_total, row_step)] = jnp.zeros((row_step,) + lhs_ref.shape[1:], jnp.bfloat16)
-    chunks = (row_total + row_step - 1) // row_step
-    behind = pl.multiple_of(chunks * ROW_CHUNK, ROW_CHUNK)
-    row_ref[pl.ds(behind, frames), :] = jnp.zeros((frames, 128), jnp.float32)
+    atom_total, frame_total, my_atoms, my_frames = carry
+    chunks = (frame_total + ROW_CHUNK - 1) // ROW_CHUNK
     width = TILE * TILE_GROUP
     groups = (atom_total + width - 1) // width
+    frame_tiles = (frame_total + 127) // 128
+
+    def build_lhs(index, carry):
+        for k in range(BUILD_GROUP):
+            tile = index * BUILD_GROUP + k
+            part = fsrc_ref[tile, 0:8]
+            last = fsrc_ref[tile, 8:9]
+            exists = fsrc_ref[tile, 9:10]
+            a = [part[k : k + 1] for k in range(3)]
+            b = [part[3 + k : 4 + k] for k in range(3)]
+            cross = [a[2] * b[1] - a[1] * b[2], a[0] * b[2] - a[2] * b[0], a[1] * b[0] - a[0] * b[1]]
+            rotations = (part[0:3], part[3:6], jnp.concatenate(cross, axis=0))
+            shifts = (part[6:7], part[7:8], last)
+            for c in range(3):
+                block = jnp.concatenate([rotations[c], rotations[c], shifts[c], exists], axis=0)
+                high, middle, low = split_rows(block)
+                ones = jnp.broadcast_to(exists, (8, 128))
+                stack = [
+                    jnp.where((sub >= 3) & (sub < 6), middle, high),
+                    jnp.where(sub < 3, low, jnp.where(sub == 6, middle, high)),
+                    jnp.where(sub < 3, middle, jnp.where(sub == 6, low, high)),
+                ]
+                stack = [x if k == c else jnp.where(sub == 7, 0.0, x) for k, x in enumerate(stack)]
+                stack.append(jnp.where((sub == c) | (sub == 3 + c), ones, 0.0))
+                stack.append(jnp.zeros((96, 128), jnp.float32))
+                turned = jnp.concatenate(stack, axis=0).T
+                lhs_ref[pl.ds(8 * tile, 8), c] = turned.astype(jnp.bfloat16).reshape(8, 16, 128)
+        return carry
+
+    build_groups = (frame_tiles + BUILD_GROUP - 1) // BUILD_GROUP
+    lax.fori_loop(0, build_groups, build_lhs, 0)
+    lhs_ref[pl.ds(build_groups * (8 * BUILD_GROUP), row_step)] = jnp.zeros((row_step,) + lhs_ref.shape[1:], jnp.bfloat16)
+    row_ref[pl.ds(pl.multiple_of(chunks * ROW_CHUNK, 8), 256), :] = jnp.zeros((256, 128), jnp.float32)
 
     def build_rhs(index, carry):
         for k in range(TILE_GROUP):
@@ -254,31 +280,33 @@
     lax.fori_loop(0, groups, build_rhs, 0)
 
     def one_chunk(chunk, carry):
-        start = pl.multiple_of(chunk * ROW_CHUNK, ROW_CHUNK)
+        start = pl.multiple_of(chunk * ROW_CHUNK, 8)
         row_ref[pl.ds(start, ROW_CHUNK), :] = jnp.zeros((ROW_CHUNK, 128), jnp.float32)
 
         def one_group(index, carry):
             lhs = lhs_ref[pl.ds(chunk * row_step, row_step)].reshape(3 * ROW_CHUNK, 128)[:, 0:32]
-            row_sums = [None] * (ROW_CHUNK // 8)
-            for k in range(TILE_GROUP):
-                tile = index * TILE_GROUP + k
-                w = jnp.dot(lhs, rhs_ref[tile], preferred_element_type=jnp.float32)
-                cap = jnp.concatenate([src_ref[tile * per_tile + m, 6:7, :] for m in range(per_tile)], axis=1)
-                cap = jnp.broadcast_to(cap * clamp_length, (8, TILE))
-                column = None
+            for pair in range(0, TILE_GROUP, 2):
+                tiles = [index * TILE_GROUP + pair + k for k in range(2)]
+                dots = [jnp.dot(lhs, rhs_ref[tile], preferred_element_type=jnp.float32) for tile in tiles]
+                caps = []
+                for tile in tiles:
+                    cap = jnp.concatenate([src_ref[tile * per_tile + m, 6:7, :] for m in range(per_tile)], axis=1)
+                    caps.append(jnp.broadcast_to(cap * clamp_length, (8, TILE)))
+                columns = [None, None]
                 for g in range(ROW_CHUNK // 8):
                     base = 48 * (g // 2) + 8 * (g % 2)
-                    w0, w1, w2 = (w[base + 16 * c : base + 16 * c + 8] for c in range(3))
-                    square = (w0 * w0 + w1 * w1) + (w2 * w2 + eps_square)
-                    distance = jnp.minimum(square * lax.rsqrt(square), cap)
-                    column = distance if column is None else column + distance
+                    row_sum = row_ref[pl.ds(start + 8 * g, 8), :]
+                    for k in range(2):
+                        w0, w1, w2 = (dots[k][base + 16 * c : base + 16 * c + 8] for c in range(3))
+                        square = (w0 * w0 + w1 * w1) + (w2 * w2 + eps_square)
+                        distance = jnp.minimum(square * lax.rsqrt(square), caps[k])
+                        columns[k] = distance if columns[k] is None else columns[k] + distance
+                        for m in range(per_tile):
+                            row_sum = row_sum + distance[:, 128 * m : 128 * m + 128]
+                    row_ref[pl.ds(start + 8 * g, 8), :] = row_sum
+                for k, tile in enumerate(tiles):
                     for m in range(per_tile):
-                        piece = distance[:, 128 * m : 128 * m + 128]
-                        row_sums[g] = piece if row_sums[g] is None else row_sums[g] + piece
-                for m in range(per_tile):
-                    col_ref[tile * per_tile + m] += column[:, 128 * m : 128 * m + 128]
-            for g in range(ROW_CHUNK // 8):
-                row_ref[pl.ds(start + 8 * g, 8), :] += row_sums[g]
+                        col_ref[tile * per_tile + m] += columns[k][:, 128 * m : 128 * m + 128]
             return carry
 
         return lax.fori_loop(0, groups, one_group, carry)
@@ -293,16 +321,16 @@
         cap = src_ref[tile, 6:7, :] * clamp_length
         return jnp.sum(col_ref[tile], axis=0, keepdims=True) - idle * jnp.minimum(least, cap)
 
-    def add_tile(tile, carry):
+    def add_group(index, carry):
         sums, floor = carry
-        return sums + col_ref[tile], floor + jnp.minimum(least, src_ref[tile, 6:7, :] * clamp_length)
-
-    sums, floor = lax.fori_loop(
-        0,
-        groups * per_tile * TILE_GROUP,
-        add_tile,
-        (jnp.zeros((8, 128), jnp.float32), jnp.zeros((1, 128), jnp.float32)),
-    )
+        for k in range(per_tile * TILE_GROUP):
+            tile = index * (per_tile * TILE_GROUP) + k
+            sums = sums + col_ref[tile]
+            floor = floor + jnp.minimum(least, src_ref[tile, 6:7, :] * clamp_length)
+        return sums, floor
+
+    empty = (jnp.zeros((8, 128), jnp.float32), jnp.zeros((1, 128), jnp.float32))
+    sums, floor = lax.fori_loop(0, groups, add_group, empty)
     loss = jnp.sum(sums, axis=0, keepdims=True) - idle * floor
     loss = jnp.sum(loss, axis=1, keepdims=True)
     atom_number = atom_total.astype(jnp.float32)
@@ -319,8 +347,14 @@
     mine = exact_dot(mine, one_hot(rank_ref[0:1, :]), 0)[0:1]
     atom_ref[...] = mine[:, :own_atoms] * scale / frame_number
 
-    rows = row_ref[pl.ds(pl.multiple_of(my_rows * 16, 16), frames), :]
-    mine = jnp.broadcast_to(jnp.sum(rows.T, axis=0, keepdims=True), (8, frames))
+    tile = my_frames // 128
+    back = (128 - my_frames % 128) % 128
+    pieces = []
+    for k in range(2):
+        rows = row_ref[pl.ds(pl.multiple_of((tile + k) * 128, 128), 128), :]
+        sums = jnp.sum(rows.T, axis=0, keepdims=True)
+        pieces.append(pltpu.roll(jnp.broadcast_to(sums, (8, 128)), back, 1))
+    mine = jnp.where(lane < 128 - my_frames % 128, pieces[0], pieces[1])
     mine = exact_dot(mine, one_hot(rank_ref[1:2, 0:frames]), 0)[0:1]
     frame_ref[...] = mine * scale / atom_number
 
@@ -336,7 +370,7 @@
     blocks, ranks = pl.pallas_call(
         prep_kernel,
         out_shape=(
-            jax.ShapeDtypeStruct((devices, 8, lanes + frames), f32),
+            jax.ShapeDtypeStruct((1, 8, lanes + frames), f32),
             jax.ShapeDtypeStruct((8, lanes), jnp.int32),
         ),
         in_specs=[HBM] * 7,
@@ -355,12 +389,17 @@
         compiler_params=pltpu.CompilerParams(vmem_limit_bytes=8 << 20),
         name="prep",
     )(*[pltpu.with_memory_space_constraint(x, pltpu.HBM) for x in inputs])
-    blocks = lax.all_to_all(blocks, ("gx", "gy"), 0, 0, tiled=True)
+    for axis, step in exchange_steps(lax.axis_size("gx"), lax.axis_size("gy")):
+        pairs = [(i, i ^ step) for i in range(lax.axis_size(axis))]
+        blocks = jnp.concatenate([blocks, lax.ppermute(blocks, axis, pairs)], axis=0)
     width = TILE * TILE_GROUP
     groups = -(-(devices * own_atoms + 256) // width)
-    row_groups = devices * (frames * USED_SLOTS // FRAME_SLOTS // 16) + 2 * ROW_CHUNK // 16
+    most = devices * (frames * USED_SLOTS // FRAME_SLOTS)
+    frame_tiles = -(-most // (128 * BUILD_GROUP)) * BUILD_GROUP + 1
+    row_groups = 8 * frame_tiles + 2 * ROW_CHUNK // 16 + 16
     scratch = [
         ((groups * width // 128, 8, 128), f32),
+        ((frame_tiles, 16, 128), f32),
         ((groups * TILE_GROUP, 32, TILE), jnp.bfloat16),
         ((row_groups, 3, 16, 128), jnp.bfloat16),
         ((row_groups * 16, 128), f32),
@@ -368,7 +407,7 @@
     ]
     room = sum(jnp.dtype(dtype).itemsize * functools.reduce(lambda a, b: a * b, shape) for shape, dtype in scratch)
     frame_loss, atom_loss, total_loss = pl.pallas_call(
-        functools.partial(pair_kernel, lax.axis_size("gy")),
+        functools.partial(pair_kernel, (lax.axis_size("gx"), lax.axis_size("gy"))),
         out_shape=(
             jax.ShapeDtypeStruct((1, frames), f32),
             jax.ShapeDtypeStruct((1, own_atoms), f32),

time: 25.7 us -> 23.4 us (0.911)
  blocking collectives: 15.9 us -> 0 us
  starting transfers between devices: 0 us -> 8.24 us
  waiting for transfers between devices: 0 us -> 6.81 us
  Pallas kernels: 8.94 us -> 7.58 us
    all_to_all x1 -> x0, blocking collectives: 15.9 us -> none  [shards(): blocks = lax.all_to_all(blocks, ('gx', 'gy'), 0, 0, tiled=True)]
    ppermute x0 -> x4, starting transfers between devices: none -> 8.24 us  [shards(): lax.ppermute(blocks, axis, pairs)]
    ppermute x0 -> x4, waiting for transfers between devices: none -> 6.81 us  [shards(): lax.ppermute(blocks, axis, pairs)]
    pallas_call x2, Pallas kernels: 8.94 us -> 7.58 us  [the longest x1 6.38 us: shards(): pl.pallas_call(functools.partial(pair_kernel, (lax.axis_size('gx'), lax.a...]
  transfers between devices with their start and end apart: 0 -> 4, of which waited for: 0 -> 4; matrix products, arithmetic and copies ran while one was open for 0% -> 0% of each run, Pallas kernels for 0% -> 0%
where the time goes in v4:
time: 23.4 us; the launch traced here: 23.3 us
  starting transfers between devices  8.24 us (35%)
  Pallas kernels  7.58 us (32%)
  waiting for transfers between devices  6.81 us (29%)
  between operations  0.67 us (3%)
    ppermute x4, starting transfers between devices, shards(): lax.ppermute(blocks, axis, pairs)  8.24 us
    ppermute x4, waiting for transfers between devices, shards(): lax.ppermute(blocks, axis, pairs)  6.81 us
    pallas_call x1, Pallas kernels, shards(): pl.pallas_call(functools.partial(pair_kernel, (lax.axis_size('gx'), lax.a...  6.38 us
    pallas_call x1, Pallas kernels, shards(): pl.pallas_call(prep_kernel, out_shape=(jax.ShapeDtypeStruct((1, 8, lanes...  1.2 us
  transfers between devices with their start and end apart: 4, of which 4 were waited for; matrix products, arithmetic and copies ran while one was open for 0% of the time, Pallas kernels for 0%

profile of v4, /device:TPU:0, one launch (start us, length us, event | category | flops | bytes accessed | tf_op | source)
XLA Modules:
  0.0 23.3 jit_solution(7562687888146730066)
XLA Ops:
  0.6 1.2 %prep.1 = (f32[1,8,384]{2,1,0:T(8,128)S(1)}, s32[8,256]{1,0:T(8,128)S(1)}) custom-call(s32[16]{0:T(128)} %refs_0_.1, s32[16]{0:T(128)} %refs_1_.1, f32[12,128]{1,0:T(8,128)} %refs_2_.1, f32[12,128]{1,0:T(8,128)} %refs_3_.1, f32[3,224]{1,0:T(4,128)} %refs_4_.1, f32[3,224]{1,0:T(4,128)} %refs_5_.1, s32[1,224]{1,0:T(1,128)} %bitcast.4), custom_call_target="tpu_custom_call" | custom-call | tf_op jit(solution)/shard_map/prep/pallas_call | solution.py:370
  1.8 3.0 %collective-permute-start = (f32[1,8,384]{2,1,0:T(8,128)S(1)}, f32[1,8,384]{2,1,0:T(8,128)S(1)}, u32[]{:S(2)}, u32[]{:S(2)}) collective-permute-start(f32[1,8,384]{2,1,0:T(8,128)S(1)} %get-tuple-element.8), channel_id=1, source_target_pairs={{0,1},{1,0},{2,3},{3,2},{4,5},{5,4},{6,7},{7,6},{8,9},{9,8},{10,11... | collective-permute-start | bytes 36872 | tf_op jit(solution)/shard_map/ppermute | solution.py:394
  4.9 1.7 %collective-permute-done = f32[1,8,384]{2,1,0:T(8,128)S(1)} collective-permute-done((f32[1,8,384]{2,1,0:T(8,128)S(1)}, f32[1,8,384]{2,1,0:T(8,128)S(1)}, u32[]{:S(2)}, u32[]{:S(2)}) %collective-permute-start) | collective-permute-done | bytes 12320 | tf_op jit(solution)/shard_map/ppermute | solution.py:394
  6.6 2.1 %collective-permute-start.1 = (f32[2,8,384]{2,1,0:T(8,128)S(1)}, f32[2,8,384]{2,1,0:T(8,128)S(1)}, u32[]{:S(2)}, u32[]{:S(2)}) collective-permute-start(f32[2,8,384]{2,1,0:T(8,128)S(1)} %pad_maximum_fusion.2), channel_id=1, source_target_pairs={{0,4},{2,6},{4,0},{6,2},{8,12},{10,14},{12,8},{14,10},{1,5},{3,7},... | collective-permute-start | bytes 73736 | tf_op jit(solution)/shard_map/ppermute | solution.py:394
  8.7 1.8 %collective-permute-done.1 = f32[2,8,384]{2,1,0:T(8,128)S(1)} collective-permute-done((f32[2,8,384]{2,1,0:T(8,128)S(1)}, f32[2,8,384]{2,1,0:T(8,128)S(1)}, u32[]{:S(2)}, u32[]{:S(2)}) %collective-permute-start.1) | collective-permute-done | bytes 24608 | tf_op jit(solution)/shard_map/ppermute | solution.py:394
  10.5 3.0 %collective-permute-start.2 = (f32[4,8,384]{2,1,0:T(8,128)S(1)}, f32[4,8,384]{2,1,0:T(8,128)S(1)}, u32[]{:S(2)}, u32[]{:S(2)}) collective-permute-start(f32[4,8,384]{2,1,0:T(8,128)S(1)} %pad_maximum_fusion.1), channel_id=1, source_target_pairs={{0,8},{2,10},{4,12},{6,14},{8,0},{10,2},{12,4},{14,6},{1,9},{3,11}... | collective-permute-start | bytes 147464 | tf_op jit(solution)/shard_map/ppermute | solution.py:394
  13.5 2.1 %collective-permute-done.2 = f32[4,8,384]{2,1,0:T(8,128)S(1)} collective-permute-done((f32[4,8,384]{2,1,0:T(8,128)S(1)}, f32[4,8,384]{2,1,0:T(8,128)S(1)}, u32[]{:S(2)}, u32[]{:S(2)}) %collective-permute-start.2) | collective-permute-done | bytes 49184 | tf_op jit(solution)/shard_map/ppermute | solution.py:394
  15.6 0.1 collective-permute-start.3
  15.7 1.3 %collective-permute-done.3 = f32[8,8,384]{2,1,0:T(8,128)S(1)} collective-permute-done((f32[8,8,384]{2,1,0:T(8,128)S(1)}, f32[8,8,384]{2,1,0:T(8,128)S(1)}, u32[]{:S(2)}, u32[]{:S(2)}) %collective-permute-start.3) | collective-permute-done | bytes 98336 | tf_op jit(solution)/shard_map/ppermute | solution.py:394
  17.0 6.4 %pairs.1 = (f32[1,128]{1,0:T(1,128)}, f32[1,224]{1,0:T(1,128)}, f32[1,1]{1,0:T(1,128)}) custom-call(f32[16,8,384]{2,1,0:T(8,128)S(1)} %constant_dynamic-update-slice_fusion.blocks_ref, s32[8,256]{1,0:T(8,128)S(1)} %get-tuple-element.9.rank_ref), custom_call_target="tpu_custom_call" | custom-call | tf_op jit(solution)/shard_map/pairs/pallas_call | solution.py:409
  (8 shorter events, 0.0 us)
Async XLA Ops:
  1.8 4.7 %collective-permute-start = (f32[1,8,384]{2,1,0:T(8,128)S(1)}, f32[1,8,384]{2,1,0:T(8,128)S(1)}, u32[]{:S(2)}, u32[]{:S(2)}) collective-permute-start(f32[1,8,384]{2,1,0:T(8,128)S(1)} %get-tuple-element.8), channel_id=1, source_target_pairs={{0,1},{1,0},{2,3},{3,2},{4,5},{5,4},{6,7},{7,6},{8,9},{9,8},{10,11... | collective-permute-start | bytes 36872 | tf_op jit(solution)/shard_map/ppermute | solution.py:394
  6.6 3.9 %collective-permute-start.1 = (f32[2,8,384]{2,1,0:T(8,128)S(1)}, f32[2,8,384]{2,1,0:T(8,128)S(1)}, u32[]{:S(2)}, u32[]{:S(2)}) collective-permute-start(f32[2,8,384]{2,1,0:T(8,128)S(1)} %pad_maximum_fusion.2), channel_id=1, source_target_pairs={{0,4},{2,6},{4,0},{6,2},{8,12},{10,14},{12,8},{14,10},{1,5},{3,7},... | collective-permute-start | bytes 73736 | tf_op jit(solution)/shard_map/ppermute | solution.py:394
  10.5 5.1 %collective-permute-start.2 = (f32[4,8,384]{2,1,0:T(8,128)S(1)}, f32[4,8,384]{2,1,0:T(8,128)S(1)}, u32[]{:S(2)}, u32[]{:S(2)}) collective-permute-start(f32[4,8,384]{2,1,0:T(8,128)S(1)} %pad_maximum_fusion.1), channel_id=1, source_target_pairs={{0,8},{2,10},{4,12},{6,14},{8,0},{10,2},{12,4},{14,6},{1,9},{3,11}... | collective-permute-start | bytes 147464 | tf_op jit(solution)/shard_map/ppermute | solution.py:394
  15.6 1.4 %collective-permute-start.3 = (f32[8,8,384]{2,1,0:T(8,128)S(1)}, f32[8,8,384]{2,1,0:T(8,128)S(1)}, u32[]{:S(2)}, u32[]{:S(2)}) collective-permute-start(f32[8,8,384]{2,1,0:T(8,128)S(1)} %pad_maximum_fusion), channel_id=1, source_target_pairs={{0,2},{2,0},{4,6},{6,4},{8,10},{10,8},{12,14},{14,12},{1,3},{3,1},... | collective-permute-start | bytes 294920 | tf_op jit(solution)/shard_map/ppermute | solution.py:394

commit v5 on v4

--- a/solution.py
+++ b/solution.py
@@ -14,11 +14,11 @@
 CHI_COUNTS = (0, 4, 2, 2, 1, 3, 3, 0, 2, 2, 2, 4, 3, 2, 2, 1, 1, 2, 2, 1)
 FRAME_SLOTS = 8
 USED_SLOTS = 6
-BUILD_GROUP = 4
+BUILD_GROUP = 8
 ATOM_SLOTS = 14
-ROW_CHUNK = 352
+ROW_CHUNK = 528
 TILE = 256
-TILE_GROUP = 4
+TILE_GROUP = 8
 VMEM = pl.BlockSpec(memory_space=pltpu.VMEM)
 HBM = pl.BlockSpec(memory_space=pltpu.HBM)
 

time: 23.4 us -> 22.6 us (0.966)
  Pallas kernels: 7.58 us -> 6.99 us
    pallas_call x1, Pallas kernels: 6.38 us -> 5.79 us  [shards(): pl.pallas_call(functools.partial(pair_kernel, (lax.axis_size('gx'), lax.a...]
where the time goes in v5:
time: 22.6 us; the launch traced here: 22.8 us
  starting transfers between devices  8.24 us (36%)
  Pallas kernels  6.99 us (31%)
  waiting for transfers between devices  6.81 us (30%)
  between operations  0.67 us (3%)
    ppermute x4, starting transfers between devices, shards(): lax.ppermute(blocks, axis, pairs)  8.24 us
    ppermute x4, waiting for transfers between devices, shards(): lax.ppermute(blocks, axis, pairs)  6.81 us
    pallas_call x1, Pallas kernels, shards(): pl.pallas_call(functools.partial(pair_kernel, (lax.axis_size('gx'), lax.a...  5.79 us
    pallas_call x1, Pallas kernels, shards(): pl.pallas_call(prep_kernel, out_shape=(jax.ShapeDtypeStruct((1, 8, lanes...  1.2 us
  transfers between devices with their start and end apart: 4, of which 4 were waited for; matrix products, arithmetic and copies ran while one was open for 0% of the time, Pallas kernels for 0%

profile of v5, /device:TPU:0, one launch (start us, length us, event | category | flops | bytes accessed | tf_op | source)
XLA Modules:
  0.0 22.8 jit_solution(9901404810306922463)
XLA Ops:
  0.6 1.2 %prep.1 = (f32[1,8,384]{2,1,0:T(8,128)S(1)}, s32[8,256]{1,0:T(8,128)S(1)}) custom-call(s32[16]{0:T(128)} %refs_0_.1, s32[16]{0:T(128)} %refs_1_.1, f32[12,128]{1,0:T(8,128)} %refs_2_.1, f32[12,128]{1,0:T(8,128)} %refs_3_.1, f32[3,224]{1,0:T(4,128)} %refs_4_.1, f32[3,224]{1,0:T(4,128)} %refs_5_.1, s32[1,224]{1,0:T(1,128)} %bitcast.4), custom_call_target="tpu_custom_call" | custom-call | tf_op jit(solution)/shard_map/prep/pallas_call | solution.py:370
  1.8 3.0 %collective-permute-start = (f32[1,8,384]{2,1,0:T(8,128)S(1)}, f32[1,8,384]{2,1,0:T(8,128)S(1)}, u32[]{:S(2)}, u32[]{:S(2)}) collective-permute-start(f32[1,8,384]{2,1,0:T(8,128)S(1)} %get-tuple-element.8), channel_id=1, source_target_pairs={{0,1},{1,0},{2,3},{3,2},{4,5},{5,4},{6,7},{7,6},{8,9},{9,8},{10,11... | collective-permute-start | bytes 36872 | tf_op jit(solution)/shard_map/ppermute | solution.py:394
  4.9 1.7 %collective-permute-done = f32[1,8,384]{2,1,0:T(8,128)S(1)} collective-permute-done((f32[1,8,384]{2,1,0:T(8,128)S(1)}, f32[1,8,384]{2,1,0:T(8,128)S(1)}, u32[]{:S(2)}, u32[]{:S(2)}) %collective-permute-start) | collective-permute-done | bytes 12320 | tf_op jit(solution)/shard_map/ppermute | solution.py:394
  6.6 2.1 %collective-permute-start.1 = (f32[2,8,384]{2,1,0:T(8,128)S(1)}, f32[2,8,384]{2,1,0:T(8,128)S(1)}, u32[]{:S(2)}, u32[]{:S(2)}) collective-permute-start(f32[2,8,384]{2,1,0:T(8,128)S(1)} %pad_maximum_fusion.2), channel_id=1, source_target_pairs={{0,4},{2,6},{4,0},{6,2},{8,12},{10,14},{12,8},{14,10},{1,5},{3,7},... | collective-permute-start | bytes 73736 | tf_op jit(solution)/shard_map/ppermute | solution.py:394
  8.7 1.8 %collective-permute-done.1 = f32[2,8,384]{2,1,0:T(8,128)S(1)} collective-permute-done((f32[2,8,384]{2,1,0:T(8,128)S(1)}, f32[2,8,384]{2,1,0:T(8,128)S(1)}, u32[]{:S(2)}, u32[]{:S(2)}) %collective-permute-start.1) | collective-permute-done | bytes 24608 | tf_op jit(solution)/shard_map/ppermute | solution.py:394
  10.5 3.0 %collective-permute-start.2 = (f32[4,8,384]{2,1,0:T(8,128)S(1)}, f32[4,8,384]{2,1,0:T(8,128)S(1)}, u32[]{:S(2)}, u32[]{:S(2)}) collective-permute-start(f32[4,8,384]{2,1,0:T(8,128)S(1)} %pad_maximum_fusion.1), channel_id=1, source_target_pairs={{0,8},{2,10},{4,12},{6,14},{8,0},{10,2},{12,4},{14,6},{1,9},{3,11}... | collective-permute-start | bytes 147464 | tf_op jit(solution)/shard_map/ppermute | solution.py:394
  13.5 2.1 %collective-permute-done.2 = f32[4,8,384]{2,1,0:T(8,128)S(1)} collective-permute-done((f32[4,8,384]{2,1,0:T(8,128)S(1)}, f32[4,8,384]{2,1,0:T(8,128)S(1)}, u32[]{:S(2)}, u32[]{:S(2)}) %collective-permute-start.2) | collective-permute-done | bytes 49184 | tf_op jit(solution)/shard_map/ppermute | solution.py:394
  15.6 0.1 collective-permute-start.3
  15.7 1.3 %collective-permute-done.3 = f32[8,8,384]{2,1,0:T(8,128)S(1)} collective-permute-done((f32[8,8,384]{2,1,0:T(8,128)S(1)}, f32[8,8,384]{2,1,0:T(8,128)S(1)}, u32[]{:S(2)}, u32[]{:S(2)}) %collective-permute-start.3) | collective-permute-done | bytes 98336 | tf_op jit(solution)/shard_map/ppermute | solution.py:394
  17.0 5.8 %pairs.1 = (f32[1,128]{1,0:T(1,128)}, f32[1,224]{1,0:T(1,128)}, f32[1,1]{1,0:T(1,128)}) custom-call(f32[16,8,384]{2,1,0:T(8,128)S(1)} %constant_dynamic-update-slice_fusion.blocks_ref, s32[8,256]{1,0:T(8,128)S(1)} %get-tuple-element.9.rank_ref), custom_call_target="tpu_custom_call" | custom-call | tf_op jit(solution)/shard_map/pairs/pallas_call | solution.py:409
  (8 shorter events, 0.0 us)
Async XLA Ops:
  1.8 4.7 %collective-permute-start = (f32[1,8,384]{2,1,0:T(8,128)S(1)}, f32[1,8,384]{2,1,0:T(8,128)S(1)}, u32[]{:S(2)}, u32[]{:S(2)}) collective-permute-start(f32[1,8,384]{2,1,0:T(8,128)S(1)} %get-tuple-element.8), channel_id=1, source_target_pairs={{0,1},{1,0},{2,3},{3,2},{4,5},{5,4},{6,7},{7,6},{8,9},{9,8},{10,11... | collective-permute-start | bytes 36872 | tf_op jit(solution)/shard_map/ppermute | solution.py:394
  6.6 3.9 %collective-permute-start.1 = (f32[2,8,384]{2,1,0:T(8,128)S(1)}, f32[2,8,384]{2,1,0:T(8,128)S(1)}, u32[]{:S(2)}, u32[]{:S(2)}) collective-permute-start(f32[2,8,384]{2,1,0:T(8,128)S(1)} %pad_maximum_fusion.2), channel_id=1, source_target_pairs={{0,4},{2,6},{4,0},{6,2},{8,12},{10,14},{12,8},{14,10},{1,5},{3,7},... | collective-permute-start | bytes 73736 | tf_op jit(solution)/shard_map/ppermute | solution.py:394
  10.5 5.1 %collective-permute-start.2 = (f32[4,8,384]{2,1,0:T(8,128)S(1)}, f32[4,8,384]{2,1,0:T(8,128)S(1)}, u32[]{:S(2)}, u32[]{:S(2)}) collective-permute-start(f32[4,8,384]{2,1,0:T(8,128)S(1)} %pad_maximum_fusion.1), channel_id=1, source_target_pairs={{0,8},{2,10},{4,12},{6,14},{8,0},{10,2},{12,4},{14,6},{1,9},{3,11}... | collective-permute-start | bytes 147464 | tf_op jit(solution)/shard_map/ppermute | solution.py:394
  15.6 1.4 %collective-permute-start.3 = (f32[8,8,384]{2,1,0:T(8,128)S(1)}, f32[8,8,384]{2,1,0:T(8,128)S(1)}, u32[]{:S(2)}, u32[]{:S(2)}) collective-permute-start(f32[8,8,384]{2,1,0:T(8,128)S(1)} %pad_maximum_fusion), channel_id=1, source_target_pairs={{0,2},{2,0},{4,6},{6,4},{8,10},{10,8},{12,14},{14,12},{1,3},{3,1},... | collective-permute-start | bytes 294920 | tf_op jit(solution)/shard_map/ppermute | solution.py:394

commit v6 on v4

--- a/solution.py
+++ b/solution.py
@@ -16,7 +16,7 @@
 USED_SLOTS = 6
 BUILD_GROUP = 4
 ATOM_SLOTS = 14
-ROW_CHUNK = 352
+ROW_CHUNK = 544
 TILE = 256
 TILE_GROUP = 4
 VMEM = pl.BlockSpec(memory_space=pltpu.VMEM)
@@ -170,26 +170,18 @@
     return code
 
 
-def pair_kernel(
-    sizes, blocks_ref, rank_ref, frame_ref, atom_ref, total_ref, src_ref, fsrc_ref, rhs_ref, lhs_ref, row_ref, col_ref
-):
+def place_half(blocks_ref, code, src_ref, fsrc_ref):
     devices = blocks_ref.shape[0]
-    frames = frame_ref.shape[1]
-    own_atoms = atom_ref.shape[1]
-    row_step = ROW_CHUNK // 16
-    per_tile = TILE // 128
-    me = device_code(*sizes)
     lane = lax.broadcasted_iota(jnp.int32, (8, 128), 1)
     sub = lax.broadcasted_iota(jnp.int32, (8, 128), 0)
     src_ref[...] = jnp.zeros(src_ref.shape, jnp.float32)
     fsrc_ref[...] = jnp.zeros(fsrc_ref.shape, jnp.float32)
-    col_ref[...] = jnp.zeros(col_ref.shape, jnp.float32)
 
     def place_block(device, carry):
         atoms_before, frames_before, my_atoms, my_frames = carry
-        my_atoms = jnp.where(device == me, atoms_before, my_atoms)
-        my_frames = jnp.where(device == me, frames_before, my_frames)
-        block = jnp.bitwise_xor(me, device)
+        my_atoms = jnp.where(device == code, atoms_before, my_atoms)
+        my_frames = jnp.where(device == code, frames_before, my_frames)
+        block = jnp.bitwise_xor(code, device)
         frame_count = jnp.max(blocks_ref[block, 7:8, 0:1]).astype(jnp.int32)
         atom_count = jnp.max(blocks_ref[block, 7:8, 1:2]).astype(jnp.int32)
         tile = atoms_before // 128
@@ -224,16 +216,23 @@
 
     carry = (0, 0, 0, 0)
     if devices == group:
-        carry = place_group(0, carry)
-    else:
-        carry = lax.fori_loop(0, devices // group, place_group, carry)
-    atom_total, frame_total, my_atoms, my_frames = carry
-    chunks = (frame_total + ROW_CHUNK - 1) // ROW_CHUNK
+        return place_group(0, carry)
+    return lax.fori_loop(0, devices // group, place_group, carry)
+
+
+def frame_chunks(frame_total):
+    return (frame_total + ROW_CHUNK - 1) // ROW_CHUNK
+
+
+def atom_groups(atom_total):
     width = TILE * TILE_GROUP
-    groups = (atom_total + width - 1) // width
-    frame_tiles = (frame_total + 127) // 128
-
-    def build_lhs(index, carry):
+    return (atom_total + width - 1) // width
+
+
+def build_rows(fsrc_ref, lhs_ref, frame_total):
+    sub = lax.broadcasted_iota(jnp.int32, (8, 128), 0)
+
+    def build(index, carry):
         for k in range(BUILD_GROUP):
             tile = index * BUILD_GROUP + k
             part = fsrc_ref[tile, 0:8]
@@ -260,12 +259,17 @@
                 lhs_ref[pl.ds(8 * tile, 8), c] = turned.astype(jnp.bfloat16).reshape(8, 16, 128)
         return carry
 
-    build_groups = (frame_tiles + BUILD_GROUP - 1) // BUILD_GROUP
-    lax.fori_loop(0, build_groups, build_lhs, 0)
-    lhs_ref[pl.ds(build_groups * (8 * BUILD_GROUP), row_step)] = jnp.zeros((row_step,) + lhs_ref.shape[1:], jnp.bfloat16)
-    row_ref[pl.ds(pl.multiple_of(chunks * ROW_CHUNK, 8), 256), :] = jnp.zeros((256, 128), jnp.float32)
-
-    def build_rhs(index, carry):
+    step = 128 * BUILD_GROUP
+    groups = (frame_total + step - 1) // step
+    lax.fori_loop(0, groups, build, 0)
+    rows = ROW_CHUNK // 16
+    lhs_ref[pl.ds(groups * (8 * BUILD_GROUP), rows)] = jnp.zeros((rows,) + lhs_ref.shape[1:], jnp.bfloat16)
+
+
+def build_columns(src_ref, rhs_ref, atom_total):
+    per_tile = TILE // 128
+
+    def build(index, carry):
         for k in range(TILE_GROUP):
             tile = index * TILE_GROUP + k
             x = jnp.concatenate([src_ref[tile * per_tile + m] for m in range(per_tile)], axis=1)
@@ -277,11 +281,22 @@
             rhs_ref[tile] = jnp.concatenate(rows, axis=0).astype(jnp.bfloat16)
         return carry
 
-    lax.fori_loop(0, groups, build_rhs, 0)
+    lax.fori_loop(0, atom_groups(atom_total), build, 0)
+
+
+def all_pairs(lhs_ref, frame_total, rhs_ref, src_ref, atom_total, col_ref, row_ref=None, before_ref=None):
+    row_step = ROW_CHUNK // 16
+    per_tile = TILE // 128
+    col_ref[...] = jnp.zeros(col_ref.shape, jnp.float32)
+    if row_ref is not None:
+        behind = pl.multiple_of(frame_chunks(frame_total) * ROW_CHUNK, 8)
+        row_ref[pl.ds(behind, 256), :] = jnp.zeros((256, 128), jnp.float32)
 
     def one_chunk(chunk, carry):
         start = pl.multiple_of(chunk * ROW_CHUNK, 8)
-        row_ref[pl.ds(start, ROW_CHUNK), :] = jnp.zeros((ROW_CHUNK, 128), jnp.float32)
+        if row_ref is not None:
+            span = pl.ds(start, ROW_CHUNK)
+            row_ref[span, :] = jnp.zeros((ROW_CHUNK, 128), jnp.float32) if before_ref is None else before_ref[span, :]
 
         def one_group(index, carry):
             lhs = lhs_ref[pl.ds(chunk * row_step, row_step)].reshape(3 * ROW_CHUNK, 128)[:, 0:32]
@@ -295,66 +310,126 @@
                 columns = [None, None]
                 for g in range(ROW_CHUNK // 8):
                     base = 48 * (g // 2) + 8 * (g % 2)
-                    row_sum = row_ref[pl.ds(start + 8 * g, 8), :]
+                    row_sum = None if row_ref is None else row_ref[pl.ds(start + 8 * g, 8), :]
                     for k in range(2):
                         w0, w1, w2 = (dots[k][base + 16 * c : base + 16 * c + 8] for c in range(3))
                         square = (w0 * w0 + w1 * w1) + (w2 * w2 + eps_square)
                         distance = jnp.minimum(square * lax.rsqrt(square), caps[k])
                         columns[k] = distance if columns[k] is None else columns[k] + distance
-                        for m in range(per_tile):
-                            row_sum = row_sum + distance[:, 128 * m : 128 * m + 128]
-                    row_ref[pl.ds(start + 8 * g, 8), :] = row_sum
+                        if row_ref is not None:
+                            for m in range(per_tile):
+                                row_sum = row_sum + distance[:, 128 * m : 128 * m + 128]
+                    if row_ref is not None:
+                        row_ref[pl.ds(start + 8 * g, 8), :] = row_sum
                 for k, tile in enumerate(tiles):
                     for m in range(per_tile):
                         col_ref[tile * per_tile + m] += columns[k][:, 128 * m : 128 * m + 128]
             return carry
 
-        return lax.fori_loop(0, groups, one_group, carry)
-
-    lax.fori_loop(0, chunks, one_chunk, 0)
-
-    idle = (chunks * ROW_CHUNK - frame_total).astype(jnp.float32)
+        return lax.fori_loop(0, atom_groups(atom_total), one_group, carry)
+
+    lax.fori_loop(0, frame_chunks(frame_total), one_chunk, 0)
+
+
+def first_kernel(sizes, blocks_ref, src_ref, rhs_ref, lhs_ref, row_ref, col_ref, info_ref, fsrc_ref):
+    code = device_code(*sizes) & (blocks_ref.shape[0] - 1)
+    info = place_half(blocks_ref, code, src_ref, fsrc_ref)
+    build_rows(fsrc_ref, lhs_ref, info[1])
+    build_columns(src_ref, rhs_ref, info[0])
+    for k, value in enumerate(info):
+        info_ref[k : k + 1, :] = jnp.full((1, 128), value, jnp.int32)
+    all_pairs(lhs_ref, info[1], rhs_ref, src_ref, info[0], col_ref, row_ref)
+
+
+def second_kernel(
+    sizes,
+    blocks_ref,
+    rank_ref,
+    src_ref,
+    rhs_ref,
+    lhs_ref,
+    before_ref,
+    col_ref,
+    info_ref,
+    frame_ref,
+    atom_ref,
+    total_ref,
+    far_src_ref,
+    far_rhs_ref,
+    far_lhs_ref,
+    row_ref,
+    near_far_ref,
+    far_near_ref,
+    far_far_ref,
+    fsrc_ref,
+):
+    half = blocks_ref.shape[0]
+    frames = frame_ref.shape[1]
+    own_atoms = atom_ref.shape[1]
+    code = device_code(*sizes)
+    atoms, frame_total, my_atoms, my_frames = (jnp.max(info_ref[k : k + 1, 0:1]) for k in range(4))
+    far_atoms, far_frames, _, _ = place_half(blocks_ref, code & (half - 1), far_src_ref, fsrc_ref)
+    build_rows(fsrc_ref, far_lhs_ref, far_frames)
+    build_columns(far_src_ref, far_rhs_ref, far_atoms)
+    all_pairs(lhs_ref, frame_total, far_rhs_ref, far_src_ref, far_atoms, near_far_ref, row_ref, before_ref)
+    all_pairs(far_lhs_ref, far_frames, rhs_ref, src_ref, atoms, far_near_ref)
+    all_pairs(far_lhs_ref, far_frames, far_rhs_ref, far_src_ref, far_atoms, far_far_ref)
+
+    lane = lax.broadcasted_iota(jnp.int32, (8, 128), 1)
+    idle = (frame_chunks(frame_total) * ROW_CHUNK - frame_total).astype(jnp.float32)
+    far_idle = (frame_chunks(far_frames) * ROW_CHUNK - far_frames).astype(jnp.float32)
     least = jnp.full((1, 128), eps_square, jnp.float32)
     least = least * lax.rsqrt(least)
 
-    def column_sums(tile):
-        cap = src_ref[tile, 6:7, :] * clamp_length
-        return jnp.sum(col_ref[tile], axis=0, keepdims=True) - idle * jnp.minimum(least, cap)
-
-    def add_group(index, carry):
-        sums, floor = carry
-        for k in range(per_tile * TILE_GROUP):
-            tile = index * (per_tile * TILE_GROUP) + k
-            sums = sums + col_ref[tile]
-            floor = floor + jnp.minimum(least, src_ref[tile, 6:7, :] * clamp_length)
-        return sums, floor
-
-    empty = (jnp.zeros((8, 128), jnp.float32), jnp.zeros((1, 128), jnp.float32))
-    sums, floor = lax.fori_loop(0, groups, add_group, empty)
-    loss = jnp.sum(sums, axis=0, keepdims=True) - idle * floor
+    def half_sums(atom_total, atoms_ref, first_ref, second_ref):
+        def add_group(index, carry):
+            first, second, floor = carry
+            per_group = TILE // 128 * TILE_GROUP
+            for k in range(per_group):
+                tile = index * per_group + k
+                first = first + first_ref[tile]
+                second = second + second_ref[tile]
+                floor = floor + jnp.minimum(least, atoms_ref[tile, 6:7, :] * clamp_length)
+            return first, second, floor
+
+        empty = jnp.zeros((8, 128), jnp.float32)
+        carry = (empty, empty, jnp.zeros((1, 128), jnp.float32))
+        first, second, floor = lax.fori_loop(0, atom_groups(atom_total), add_group, carry)
+        first = jnp.sum(first, axis=0, keepdims=True) - idle * floor
+        return first, jnp.sum(second, axis=0, keepdims=True) - far_idle * floor
+
+    near_near, far_near = half_sums(atoms, src_ref, col_ref, far_near_ref)
+    near_far, far_far = half_sums(far_atoms, far_src_ref, near_far_ref, far_far_ref)
+    upper = code >= half
+    loss = jnp.where(upper, far_far, near_near) + jnp.where(upper, far_near, near_far)
+    loss = loss + (jnp.where(upper, near_far, far_near) + jnp.where(upper, near_near, far_far))
     loss = jnp.sum(loss, axis=1, keepdims=True)
-    atom_number = atom_total.astype(jnp.float32)
-    frame_number = frame_total.astype(jnp.float32)
+    atom_number = (atoms + far_atoms).astype(jnp.float32)
+    frame_number = (frame_total + far_frames).astype(jnp.float32)
     scale = 1.0 / clamp_length
     total_ref[...] = loss * scale / (frame_number * atom_number)
 
     tile = my_atoms // 128
     turn = my_atoms % 128
-    back = (128 - turn) % 128
-    pieces = [pltpu.roll(jnp.broadcast_to(column_sums(tile + k), (8, 128)), back, 1) for k in range(3)]
+    pieces = []
+    for k in range(3):
+        cap = src_ref[tile + k, 6:7, :] * clamp_length
+        sums = jnp.sum(col_ref[tile + k] + far_near_ref[tile + k], axis=0, keepdims=True)
+        sums = sums - (idle + far_idle) * jnp.minimum(least, cap)
+        pieces.append(pltpu.roll(jnp.broadcast_to(sums, (8, 128)), (128 - turn) % 128, 1))
     keep = lane < 128 - turn
     mine = jnp.concatenate([jnp.where(keep, pieces[k], pieces[k + 1]) for k in range(2)], axis=1)
     mine = exact_dot(mine, one_hot(rank_ref[0:1, :]), 0)[0:1]
     atom_ref[...] = mine[:, :own_atoms] * scale / frame_number
 
     tile = my_frames // 128
-    back = (128 - my_frames % 128) % 128
+    turn = my_frames % 128
     pieces = []
     for k in range(2):
         rows = row_ref[pl.ds(pl.multiple_of((tile + k) * 128, 128), 128), :]
         sums = jnp.sum(rows.T, axis=0, keepdims=True)
-        pieces.append(pltpu.roll(jnp.broadcast_to(sums, (8, 128)), back, 1))
-    mine = jnp.where(lane < 128 - my_frames % 128, pieces[0], pieces[1])
+        pieces.append(pltpu.roll(jnp.broadcast_to(sums, (8, 128)), (128 - turn) % 128, 1))
+    mine = jnp.where(lane < 128 - turn, pieces[0], pieces[1])
     mine = exact_dot(mine, one_hot(rank_ref[1:2, 0:frames]), 0)[0:1]
     frame_ref[...] = mine * scale / atom_number
 
@@ -389,36 +464,52 @@
         compiler_params=pltpu.CompilerParams(vmem_limit_bytes=8 << 20),
         name="prep",
     )(*[pltpu.with_memory_space_constraint(x, pltpu.HBM) for x in inputs])
-    for axis, step in exchange_steps(lax.axis_size("gx"), lax.axis_size("gy")):
-        pairs = [(i, i ^ step) for i in range(lax.axis_size(axis))]
-        blocks = jnp.concatenate([blocks, lax.ppermute(blocks, axis, pairs)], axis=0)
-    width = TILE * TILE_GROUP
-    groups = -(-(devices * own_atoms + 256) // width)
-    most = devices * (frames * USED_SLOTS // FRAME_SLOTS)
+    sizes = (lax.axis_size("gx"), lax.axis_size("gy"))
+    far = None
+    for axis, step in exchange_steps(*sizes):
+        if far is not None:
+            blocks = jnp.concatenate([blocks, far], axis=0)
+        far = lax.ppermute(blocks, axis, [(i, i ^ step) for i in range(lax.axis_size(axis))])
+    half = devices // 2
+    groups = -(-(half * own_atoms + 256) // (TILE * TILE_GROUP))
+    tiles = groups * TILE_GROUP * (TILE // 128)
+    most = half * (frames * USED_SLOTS // FRAME_SLOTS)
     frame_tiles = -(-most // (128 * BUILD_GROUP)) * BUILD_GROUP + 1
-    row_groups = 8 * frame_tiles + 2 * ROW_CHUNK // 16 + 16
-    scratch = [
-        ((groups * width // 128, 8, 128), f32),
-        ((frame_tiles, 16, 128), f32),
-        ((groups * TILE_GROUP, 32, TILE), jnp.bfloat16),
-        ((row_groups, 3, 16, 128), jnp.bfloat16),
-        ((row_groups * 16, 128), f32),
-        ((groups * width // 128, 8, 128), f32),
-    ]
-    room = sum(jnp.dtype(dtype).itemsize * functools.reduce(lambda a, b: a * b, shape) for shape, dtype in scratch)
+    row_groups = 8 * frame_tiles + 2 * (ROW_CHUNK // 16) + 16
+    columns = ((tiles, 8, 128), f32)
+    frame_source = ((frame_tiles, 16, 128), f32)
+    right = ((groups * TILE_GROUP, 32, TILE), jnp.bfloat16)
+    left = ((row_groups, 3, 16, 128), jnp.bfloat16)
+    rows = ((row_groups * 16, 128), f32)
+
+    def room(*arrays):
+        return sum(jnp.dtype(d).itemsize * functools.reduce(lambda a, b: a * b, shape) for shape, d in arrays)
+
+    kept = [columns, right, left, rows, columns, ((8, 128), jnp.int32)]
+    near = pl.pallas_call(
+        functools.partial(first_kernel, sizes),
+        out_shape=[jax.ShapeDtypeStruct(*x) for x in kept],
+        in_specs=[VMEM],
+        out_specs=[VMEM] * len(kept),
+        scratch_shapes=[pltpu.VMEM(*frame_source)],
+        compiler_params=pltpu.CompilerParams(vmem_limit_bytes=room(*kept, frame_source) + (8 << 20)),
+        cost_estimate=pl.CostEstimate(flops=4 * 10**9, bytes_accessed=1 << 20, transcendentals=0),
+        name="near",
+    )(blocks)
+    scratch = [columns, right, left, rows, columns, columns, columns, frame_source]
     frame_loss, atom_loss, total_loss = pl.pallas_call(
-        functools.partial(pair_kernel, (lax.axis_size("gx"), lax.axis_size("gy"))),
+        functools.partial(second_kernel, sizes),
         out_shape=(
             jax.ShapeDtypeStruct((1, frames), f32),
             jax.ShapeDtypeStruct((1, own_atoms), f32),
             jax.ShapeDtypeStruct((1, 1), f32),
         ),
-        in_specs=[VMEM, VMEM],
+        in_specs=[VMEM] * (2 + len(kept)),
         out_specs=(VMEM, VMEM, VMEM),
-        scratch_shapes=[pltpu.VMEM(shape, dtype) for shape, dtype in scratch],
-        compiler_params=pltpu.CompilerParams(vmem_limit_bytes=room + (12 << 20)),
-        name="pairs",
-    )(blocks, ranks)
+        scratch_shapes=[pltpu.VMEM(*x) for x in scratch],
+        compiler_params=pltpu.CompilerParams(vmem_limit_bytes=room(*kept, *scratch) + (8 << 20)),
+        name="rest",
+    )(far, ranks, *near)
     return (frame_loss.reshape(frames), atom_loss.reshape(own_atoms), total_loss.reshape(1))
 
 

time: 23.4 us -> 22.1 us (0.944)
  waiting for transfers between devices: 6.81 us -> 5.54 us
    ppermute x4, waiting for transfers between devices: 6.81 us -> 5.54 us  [shards(): lax.ppermute(blocks, axis, [(i, i ^ step) for i in range(lax.axis_size(ax...]
    pallas_call x1 -> x2, Pallas kernels: 6.38 us -> 6.27 us  [the longest x1 4.6 us: shards(): pl.pallas_call(functools.partial(second_kernel, sizes), out_shape=(jax.Sh...]
  transfers between devices with their start and end apart: 4 -> 4, of which waited for: 4 -> 3; matrix products, arithmetic and copies ran while one was open for 0% -> 0% of each run, Pallas kernels for 0% -> 8%
where the time goes in v6:
time: 22.1 us; the launch traced here: 21.9 us
  starting transfers between devices  8.18 us (37%)
  Pallas kernels  7.47 us (34%)
  waiting for transfers between devices  5.54 us (25%)
  between operations  0.67 us (3%)
    ppermute x4, starting transfers between devices, shards(): lax.ppermute(blocks, axis, [(i, i ^ step) for i in range(lax.axis_size(ax...  8.18 us
    ppermute x4, waiting for transfers between devices, shards(): lax.ppermute(blocks, axis, [(i, i ^ step) for i in range(lax.axis_size(ax...  5.54 us
    pallas_call x1, Pallas kernels, shards(): pl.pallas_call(functools.partial(second_kernel, sizes), out_shape=(jax.Sh...  4.6 us
    pallas_call x1, Pallas kernels, shards(): pl.pallas_call(functools.partial(first_kernel, sizes), out_shape=[jax.Sha...  1.67 us
    pallas_call x1, Pallas kernels, shards(): pl.pallas_call(prep_kernel, out_shape=(jax.ShapeDtypeStruct((1, 8, lanes...  1.2 us
  transfers between devices with their start and end apart: 4, of which 3 were waited for; matrix products, arithmetic and copies ran while one was open for 0% of the time, Pallas kernels for 8%

profile of v6, /device:TPU:0, one launch (start us, length us, event | category | flops | bytes accessed | tf_op | source)
XLA Modules:
  0.0 21.9 jit_solution(10938726552534308442)
XLA Ops:
  0.6 1.2 %prep.1 = (f32[1,8,384]{2,1,0:T(8,128)S(1)}, s32[8,256]{1,0:T(8,128)S(1)}) custom-call(s32[16]{0:T(128)} %refs_0_.1, s32[16]{0:T(128)} %refs_1_.1, f32[12,128]{1,0:T(8,128)} %refs_2_.1, f32[12,128]{1,0:T(8,128)} %refs_3_.1, f32[3,224]{1,0:T(4,128)} %refs_4_.1, f32[3,224]{1,0:T(4,128)} %refs_5_.1, s32[1,224]{1,0:T(1,128)} %bitcast.4), custom_call_target="tpu_custom_call" | custom-call | tf_op jit(solution)/shard_map/prep/pallas_call | solution.py:445
  1.8 3.0 %collective-permute-start = (f32[1,8,384]{2,1,0:T(8,128)S(1)}, f32[1,8,384]{2,1,0:T(8,128)S(1)}, u32[]{:S(2)}, u32[]{:S(2)}) collective-permute-start(f32[1,8,384]{2,1,0:T(8,128)S(1)} %get-tuple-element.14), channel_id=1, source_target_pairs={{0,1},{1,0},{2,3},{3,2},{4,5},{5,4},{6,7},{7,6},{8,9},{9,8},{10,11... | collective-permute-start | bytes 36872 | tf_op jit(solution)/shard_map/ppermute | solution.py:472
  4.9 1.7 %collective-permute-done = f32[1,8,384]{2,1,0:T(8,128)S(1)} collective-permute-done((f32[1,8,384]{2,1,0:T(8,128)S(1)}, f32[1,8,384]{2,1,0:T(8,128)S(1)}, u32[]{:S(2)}, u32[]{:S(2)}) %collective-permute-start) | collective-permute-done | bytes 12320 | tf_op jit(solution)/shard_map/ppermute | solution.py:472
  6.6 2.1 %collective-permute-start.1 = (f32[2,8,384]{2,1,0:T(8,128)S(1)}, f32[2,8,384]{2,1,0:T(8,128)S(1)}, u32[]{:S(2)}, u32[]{:S(2)}) collective-permute-start(f32[2,8,384]{2,1,0:T(8,128)S(1)} %pad_maximum_fusion.1), channel_id=1, source_target_pairs={{0,4},{2,6},{4,0},{6,2},{8,12},{10,14},{12,8},{14,10},{1,5},{3,7},... | collective-permute-start | bytes 73736 | tf_op jit(solution)/shard_map/ppermute | solution.py:472
  8.7 1.8 %collective-permute-done.1 = f32[2,8,384]{2,1,0:T(8,128)S(1)} collective-permute-done((f32[2,8,384]{2,1,0:T(8,128)S(1)}, f32[2,8,384]{2,1,0:T(8,128)S(1)}, u32[]{:S(2)}, u32[]{:S(2)}) %collective-permute-start.1) | collective-permute-done | bytes 24608 | tf_op jit(solution)/shard_map/ppermute | solution.py:472
  10.5 3.0 %collective-permute-start.2 = (f32[4,8,384]{2,1,0:T(8,128)S(1)}, f32[4,8,384]{2,1,0:T(8,128)S(1)}, u32[]{:S(2)}, u32[]{:S(2)}) collective-permute-start(f32[4,8,384]{2,1,0:T(8,128)S(1)} %pad_maximum_fusion), channel_id=1, source_target_pairs={{0,8},{2,10},{4,12},{6,14},{8,0},{10,2},{12,4},{14,6},{1,9},{3,11}... | collective-permute-start | bytes 147464 | tf_op jit(solution)/shard_map/ppermute | solution.py:472
  13.5 2.1 %collective-permute-done.2 = f32[4,8,384]{2,1,0:T(8,128)S(1)} collective-permute-done((f32[4,8,384]{2,1,0:T(8,128)S(1)}, f32[4,8,384]{2,1,0:T(8,128)S(1)}, u32[]{:S(2)}, u32[]{:S(2)}) %collective-permute-start.2) | collective-permute-done | bytes 49184 | tf_op jit(solution)/shard_map/ppermute | solution.py:472
  15.6 0.0 collective-permute-start.3
  15.6 1.7 %near.1 = (f32[16,8,128]{2,1,0:T(8,128)S(1)}, bf16[8,32,256]{2,1,0:T(8,128)(2,1)S(1)}, bf16[156,3,16,128]{3,2,1,0:T(8,128)(2,1)S(1)}, f32[2496,128]{1,0:T(8,128)...) custom-call(f32[8,8,384]{2,1,0:T(8,128)S(1)} %constant_dynamic-update-slice_fusion.blocks_ref), custom_call_target="tpu_custom_call" | custom-call | flops 4000000000 | bytes 1048576 | tf_op jit(solution)/shard_map/near/pallas_call | solution.py:489
  17.3 0.0 collective-permute-done.3.blocks_ref
  17.3 4.6 %rest.1 = (f32[1,128]{1,0:T(1,128)}, f32[1,224]{1,0:T(1,128)}, f32[1,1]{1,0:T(1,128)}) custom-call(f32[8,8,384]{2,1,0:T(8,128)S(1)} %collective-permute-done.3.blocks_ref, s32[8,256]{1,0:T(8,128)S(1)} %get-tuple-element.15.rank_ref, f32[16,8,128]{2,1,0:T(8,128)S(1)} %get-tuple-element.16.src_ref, bf16[8,32,256]{2,1,0:T(8,128)(2,1)S(1)} %get-tuple-element.17.rhs_ref, ...), custom_call_target="tpu_custom_call" | custom-call | tf_op jit(solution)/shard_map/rest/pallas_call | solution.py:500
  (6 shorter events, 0.0 us)
Async XLA Ops:
  1.8 4.7 %collective-permute-start = (f32[1,8,384]{2,1,0:T(8,128)S(1)}, f32[1,8,384]{2,1,0:T(8,128)S(1)}, u32[]{:S(2)}, u32[]{:S(2)}) collective-permute-start(f32[1,8,384]{2,1,0:T(8,128)S(1)} %get-tuple-element.14), channel_id=1, source_target_pairs={{0,1},{1,0},{2,3},{3,2},{4,5},{5,4},{6,7},{7,6},{8,9},{9,8},{10,11... | collective-permute-start | bytes 36872 | tf_op jit(solution)/shard_map/ppermute | solution.py:472
  6.6 3.9 %collective-permute-start.1 = (f32[2,8,384]{2,1,0:T(8,128)S(1)}, f32[2,8,384]{2,1,0:T(8,128)S(1)}, u32[]{:S(2)}, u32[]{:S(2)}) collective-permute-start(f32[2,8,384]{2,1,0:T(8,128)S(1)} %pad_maximum_fusion.1), channel_id=1, source_target_pairs={{0,4},{2,6},{4,0},{6,2},{8,12},{10,14},{12,8},{14,10},{1,5},{3,7},... | collective-permute-start | bytes 73736 | tf_op jit(solution)/shard_map/ppermute | solution.py:472
  10.5 5.1 %collective-permute-start.2 = (f32[4,8,384]{2,1,0:T(8,128)S(1)}, f32[4,8,384]{2,1,0:T(8,128)S(1)}, u32[]{:S(2)}, u32[]{:S(2)}) collective-permute-start(f32[4,8,384]{2,1,0:T(8,128)S(1)} %pad_maximum_fusion), channel_id=1, source_target_pairs={{0,8},{2,10},{4,12},{6,14},{8,0},{10,2},{12,4},{14,6},{1,9},{3,11}... | collective-permute-start | bytes 147464 | tf_op jit(solution)/shard_map/ppermute | solution.py:472
  15.6 1.7 %collective-permute-start.3 = (f32[8,8,384]{2,1,0:T(8,128)S(1)}, f32[8,8,384]{2,1,0:T(8,128)S(1)}, u32[]{:S(2)}, u32[]{:S(2)}) collective-permute-start(f32[8,8,384]{2,1,0:T(8,128)S(1)} %constant_dynamic-update-slice_fusion.blocks_ref), channel_id=1, source_target_pairs={{0,2},{2,0},{4,6},{6,4},{8,10},{10,8},{12,14},{14,12},{1,3},{3,1},... | collective-permute-start | bytes 294920 | tf_op jit(solution)/shard_map/ppermute | solution.py:472

commit v7 on v6

--- a/solution.py
+++ b/solution.py
@@ -331,7 +331,31 @@
     lax.fori_loop(0, frame_chunks(frame_total), one_chunk, 0)
 
 
-def first_kernel(sizes, blocks_ref, src_ref, rhs_ref, lhs_ref, row_ref, col_ref, info_ref, fsrc_ref):
+def idle_rows(frame_total):
+    return (frame_chunks(frame_total) * ROW_CHUNK - frame_total).astype(jnp.float32)
+
+
+def least_distance():
+    square = jnp.full((1, 128), eps_square, jnp.float32)
+    return square * lax.rsqrt(square)
+
+
+def column_total(atom_total, src_ref, col_ref, idle):
+    def add_group(index, carry):
+        sums, floor = carry
+        per_group = TILE // 128 * TILE_GROUP
+        for k in range(per_group):
+            tile = index * per_group + k
+            sums = sums + col_ref[tile]
+            floor = floor + jnp.minimum(least_distance(), src_ref[tile, 6:7, :] * clamp_length)
+        return sums, floor
+
+    carry = (jnp.zeros((8, 128), jnp.float32), jnp.zeros((1, 128), jnp.float32))
+    sums, floor = lax.fori_loop(0, atom_groups(atom_total), add_group, carry)
+    return jnp.sum(sums, axis=0, keepdims=True) - idle * floor
+
+
+def first_kernel(sizes, blocks_ref, loss_ref, src_ref, rhs_ref, lhs_ref, row_ref, col_ref, info_ref, fsrc_ref):
     code = device_code(*sizes) & (blocks_ref.shape[0] - 1)
     info = place_half(blocks_ref, code, src_ref, fsrc_ref)
     build_rows(fsrc_ref, lhs_ref, info[1])
@@ -339,6 +363,8 @@
     for k, value in enumerate(info):
         info_ref[k : k + 1, :] = jnp.full((1, 128), value, jnp.int32)
     all_pairs(lhs_ref, info[1], rhs_ref, src_ref, info[0], col_ref, row_ref)
+    loss = column_total(info[0], src_ref, col_ref, idle_rows(info[1]))
+    loss_ref[...] = jnp.broadcast_to(loss, loss_ref.shape)
 
 
 def second_kernel(
@@ -353,14 +379,13 @@
     info_ref,
     frame_ref,
     atom_ref,
-    total_ref,
+    cross_ref,
     far_src_ref,
     far_rhs_ref,
     far_lhs_ref,
     row_ref,
     near_far_ref,
     far_near_ref,
-    far_far_ref,
     fsrc_ref,
 ):
     half = blocks_ref.shape[0]
@@ -373,41 +398,20 @@
     build_columns(far_src_ref, far_rhs_ref, far_atoms)
     all_pairs(lhs_ref, frame_total, far_rhs_ref, far_src_ref, far_atoms, near_far_ref, row_ref, before_ref)
     all_pairs(far_lhs_ref, far_frames, rhs_ref, src_ref, atoms, far_near_ref)
-    all_pairs(far_lhs_ref, far_frames, far_rhs_ref, far_src_ref, far_atoms, far_far_ref)
 
     lane = lax.broadcasted_iota(jnp.int32, (8, 128), 1)
-    idle = (frame_chunks(frame_total) * ROW_CHUNK - frame_total).astype(jnp.float32)
-    far_idle = (frame_chunks(far_frames) * ROW_CHUNK - far_frames).astype(jnp.float32)
-    least = jnp.full((1, 128), eps_square, jnp.float32)
-    least = least * lax.rsqrt(least)
-
-    def half_sums(atom_total, atoms_ref, first_ref, second_ref):
-        def add_group(index, carry):
-            first, second, floor = carry
-            per_group = TILE // 128 * TILE_GROUP
-            for k in range(per_group):
-                tile = index * per_group + k
-                first = first + first_ref[tile]
-                second = second + second_ref[tile]
-                floor = floor + jnp.minimum(least, atoms_ref[tile, 6:7, :] * clamp_length)
-            return first, second, floor
-
-        empty = jnp.zeros((8, 128), jnp.float32)
-        carry = (empty, empty, jnp.zeros((1, 128), jnp.float32))
-        first, second, floor = lax.fori_loop(0, atom_groups(atom_total), add_group, carry)
-        first = jnp.sum(first, axis=0, keepdims=True) - idle * floor
-        return first, jnp.sum(second, axis=0, keepdims=True) - far_idle * floor
-
-    near_near, far_near = half_sums(atoms, src_ref, col_ref, far_near_ref)
-    near_far, far_far = half_sums(far_atoms, far_src_ref, near_far_ref, far_far_ref)
-    upper = code >= half
-    loss = jnp.where(upper, far_far, near_near) + jnp.where(upper, far_near, near_far)
-    loss = loss + (jnp.where(upper, near_far, far_near) + jnp.where(upper, near_near, far_far))
-    loss = jnp.sum(loss, axis=1, keepdims=True)
+    idle = idle_rows(frame_total)
+    far_idle = idle_rows(far_frames)
+    least = least_distance()
+    near_far = column_total(far_atoms, far_src_ref, near_far_ref, idle)
+    far_near = column_total(atoms, src_ref, far_near_ref, far_idle)
     atom_number = (atoms + far_atoms).astype(jnp.float32)
     frame_number = (frame_total + far_frames).astype(jnp.float32)
     scale = 1.0 / clamp_length
-    total_ref[...] = loss * scale / (frame_number * atom_number)
+    upper = code >= half
+    cross_ref[0:1, :] = jnp.where(upper, far_near, near_far)
+    cross_ref[1:2, :] = jnp.where(upper, near_far, far_near)
+    cross_ref[2:3, :] = jnp.full((1, 128), scale, jnp.float32) / (frame_number * atom_number)
 
     tile = my_atoms // 128
     turn = my_atoms % 128
@@ -432,6 +436,17 @@
     mine = jnp.where(lane < 128 - turn, pieces[0], pieces[1])
     mine = exact_dot(mine, one_hot(rank_ref[1:2, 0:frames]), 0)[0:1]
     frame_ref[...] = mine * scale / atom_number
+
+
+def finish_kernel(sizes, near_ref, far_ref, cross_ref, frames_ref, atoms_ref, frame_ref, atom_ref, total_ref):
+    upper = (device_code(*sizes) * 2) // (sizes[0] * sizes[1]) == 1
+    near = near_ref[0:1, :]
+    far = far_ref[0:1, :]
+    loss = jnp.where(upper, far, near) + cross_ref[0:1, :]
+    loss = loss + (cross_ref[1:2, :] + jnp.where(upper, near, far))
+    total_ref[...] = jnp.sum(loss, axis=1, keepdims=True) * cross_ref[2:3, 0:1]
+    frame_ref[...] = frames_ref[...]
+    atom_ref[...] = atoms_ref[...]
 
 
 def shards(pred_frames, true_frames, pred_atoms, true_atoms, atom_mask, residue_types, swap_flags):
@@ -485,8 +500,8 @@
     def room(*arrays):
         return sum(jnp.dtype(d).itemsize * functools.reduce(lambda a, b: a * b, shape) for shape, d in arrays)
 
-    kept = [columns, right, left, rows, columns, ((8, 128), jnp.int32)]
-    near = pl.pallas_call(
+    kept = [((8, 128), f32), columns, right, left, rows, columns, ((8, 128), jnp.int32)]
+    loss, *near = pl.pallas_call(
         functools.partial(first_kernel, sizes),
         out_shape=[jax.ShapeDtypeStruct(*x) for x in kept],
         in_specs=[VMEM],
@@ -496,20 +511,27 @@
         cost_estimate=pl.CostEstimate(flops=4 * 10**9, bytes_accessed=1 << 20, transcendentals=0),
         name="near",
     )(blocks)
-    scratch = [columns, right, left, rows, columns, columns, columns, frame_source]
-    frame_loss, atom_loss, total_loss = pl.pallas_call(
+    far_loss = lax.ppermute(loss, axis, [(i, i ^ step) for i in range(lax.axis_size(axis))])
+    scratch = [columns, right, left, rows, columns, columns, frame_source]
+    results = [((1, frames), f32), ((1, own_atoms), f32)]
+    frame_loss, atom_loss, cross = pl.pallas_call(
         functools.partial(second_kernel, sizes),
-        out_shape=(
-            jax.ShapeDtypeStruct((1, frames), f32),
-            jax.ShapeDtypeStruct((1, own_atoms), f32),
-            jax.ShapeDtypeStruct((1, 1), f32),
-        ),
-        in_specs=[VMEM] * (2 + len(kept)),
-        out_specs=(VMEM, VMEM, VMEM),
+        out_shape=[jax.ShapeDtypeStruct(*x) for x in results + [((8, 128), f32)]],
+        in_specs=[VMEM] * (1 + len(kept)),
+        out_specs=[VMEM] * 3,
         scratch_shapes=[pltpu.VMEM(*x) for x in scratch],
         compiler_params=pltpu.CompilerParams(vmem_limit_bytes=room(*kept, *scratch) + (8 << 20)),
+        cost_estimate=pl.CostEstimate(flops=8 * 10**9, bytes_accessed=1 << 20, transcendentals=0),
         name="rest",
     )(far, ranks, *near)
+    frame_loss, atom_loss, total_loss = pl.pallas_call(
+        functools.partial(finish_kernel, sizes),
+        out_shape=[jax.ShapeDtypeStruct(*x) for x in results + [((1, 1), f32)]],
+        in_specs=[VMEM] * 5,
+        out_specs=[VMEM] * 3,
+        compiler_params=pltpu.CompilerParams(vmem_limit_bytes=8 << 20),
+        name="finish",
+    )(loss, far_loss, cross, frame_loss, atom_loss)
     return (frame_loss.reshape(frames), atom_loss.reshape(own_atoms), total_loss.reshape(1))
 
 

time: 22.1 us -> 21.7 us (0.982)
  Pallas kernels: 7.47 us -> 6.56 us
  starting transfers between devices: 8.18 us -> 8.73 us
    pallas_call x1 -> x2, Pallas kernels: 4.6 us -> 3.66 us  [the longest x1 3.03 us: shards(): pl.pallas_call(functools.partial(second_kernel, sizes), out_shape=[jax.Sh...]
    ppermute x0 -> x1, starting transfers between devices: none -> 0.56 us  [shards(): lax.ppermute(loss, axis, [(i, i ^ step) for i in range(lax.axis_size(axis...]
  transfers between devices with their start and end apart: 4 -> 5, of which waited for: 3 -> 3; matrix products, arithmetic and copies ran while one was open for 0% -> 0% of each run, Pallas kernels for 8% -> 22%
where the time goes in v7:
time: 21.7 us; the launch traced here: 21.5 us
  starting transfers between devices  8.73 us (40%)
  Pallas kernels  6.56 us (30%)
  waiting for transfers between devices  5.54 us (26%)
  between operations  0.66 us (3%)
    ppermute x4, starting transfers between devices, shards(): lax.ppermute(blocks, axis, [(i, i ^ step) for i in range(lax.axis_size(ax...  8.18 us
    ppermute x4, waiting for transfers between devices, shards(): lax.ppermute(blocks, axis, [(i, i ^ step) for i in range(lax.axis_size(ax...  5.54 us
    pallas_call x1, Pallas kernels, shards(): pl.pallas_call(functools.partial(second_kernel, sizes), out_shape=[jax.Sh...  3.03 us
    pallas_call x1, Pallas kernels, shards(): pl.pallas_call(functools.partial(first_kernel, sizes), out_shape=[jax.Sha...  1.7 us
    pallas_call x1, Pallas kernels, shards(): pl.pallas_call(prep_kernel, out_shape=(jax.ShapeDtypeStruct((1, 8, lanes...  1.2 us
    pallas_call x1, Pallas kernels, shards(): pl.pallas_call(functools.partial(finish_kernel, sizes), out_shape=[jax.Sh...  0.63 us
    ppermute x1, starting transfers between devices, shards(): lax.ppermute(loss, axis, [(i, i ^ step) for i in range(lax.axis_size(axis...  0.56 us
  transfers between devices with their start and end apart: 5, of which 3 were waited for; matrix products, arithmetic and copies ran while one was open for 0% of the time, Pallas kernels for 22%

profile of v7, /device:TPU:0, one launch (start us, length us, event | category | flops | bytes accessed | tf_op | source)
XLA Modules:
  0.0 21.5 jit_solution(6856283996152722390)
XLA Ops:
  0.6 1.2 %prep.1 = (f32[1,8,384]{2,1,0:T(8,128)S(1)}, s32[8,256]{1,0:T(8,128)S(1)}) custom-call(s32[16]{0:T(128)} %refs_0_.1, s32[16]{0:T(128)} %refs_1_.1, f32[12,128]{1,0:T(8,128)} %refs_2_.1, f32[12,128]{1,0:T(8,128)} %refs_3_.1, f32[3,224]{1,0:T(4,128)} %refs_4_.1, f32[3,224]{1,0:T(4,128)} %refs_5_.1, s32[1,224]{1,0:T(1,128)} %bitcast.4), custom_call_target="tpu_custom_call" | custom-call | tf_op jit(solution)/shard_map/prep/pallas_call | solution.py:460
  1.8 3.0 %collective-permute-start = (f32[1,8,384]{2,1,0:T(8,128)S(1)}, f32[1,8,384]{2,1,0:T(8,128)S(1)}, u32[]{:S(2)}, u32[]{:S(2)}) collective-permute-start(f32[1,8,384]{2,1,0:T(8,128)S(1)} %get-tuple-element.18), channel_id=1, source_target_pairs={{0,1},{1,0},{2,3},{3,2},{4,5},{5,4},{6,7},{7,6},{8,9},{9,8},{10,11... | collective-permute-start | bytes 36872 | tf_op jit(solution)/shard_map/ppermute | solution.py:487
  4.9 1.7 %collective-permute-done = f32[1,8,384]{2,1,0:T(8,128)S(1)} collective-permute-done((f32[1,8,384]{2,1,0:T(8,128)S(1)}, f32[1,8,384]{2,1,0:T(8,128)S(1)}, u32[]{:S(2)}, u32[]{:S(2)}) %collective-permute-start) | collective-permute-done | bytes 12320 | tf_op jit(solution)/shard_map/ppermute | solution.py:487
  6.6 2.1 %collective-permute-start.1 = (f32[2,8,384]{2,1,0:T(8,128)S(1)}, f32[2,8,384]{2,1,0:T(8,128)S(1)}, u32[]{:S(2)}, u32[]{:S(2)}) collective-permute-start(f32[2,8,384]{2,1,0:T(8,128)S(1)} %pad_maximum_fusion.1), channel_id=1, source_target_pairs={{0,4},{2,6},{4,0},{6,2},{8,12},{10,14},{12,8},{14,10},{1,5},{3,7},... | collective-permute-start | bytes 73736 | tf_op jit(solution)/shard_map/ppermute | solution.py:487
  8.7 1.8 %collective-permute-done.1 = f32[2,8,384]{2,1,0:T(8,128)S(1)} collective-permute-done((f32[2,8,384]{2,1,0:T(8,128)S(1)}, f32[2,8,384]{2,1,0:T(8,128)S(1)}, u32[]{:S(2)}, u32[]{:S(2)}) %collective-permute-start.1) | collective-permute-done | bytes 24608 | tf_op jit(solution)/shard_map/ppermute | solution.py:487
  10.5 3.0 %collective-permute-start.2 = (f32[4,8,384]{2,1,0:T(8,128)S(1)}, f32[4,8,384]{2,1,0:T(8,128)S(1)}, u32[]{:S(2)}, u32[]{:S(2)}) collective-permute-start(f32[4,8,384]{2,1,0:T(8,128)S(1)} %pad_maximum_fusion), channel_id=1, source_target_pairs={{0,8},{2,10},{4,12},{6,14},{8,0},{10,2},{12,4},{14,6},{1,9},{3,11}... | collective-permute-start | bytes 147464 | tf_op jit(solution)/shard_map/ppermute | solution.py:487
  13.5 2.1 %collective-permute-done.2 = f32[4,8,384]{2,1,0:T(8,128)S(1)} collective-permute-done((f32[4,8,384]{2,1,0:T(8,128)S(1)}, f32[4,8,384]{2,1,0:T(8,128)S(1)}, u32[]{:S(2)}, u32[]{:S(2)}) %collective-permute-start.2) | collective-permute-done | bytes 49184 | tf_op jit(solution)/shard_map/ppermute | solution.py:487
  15.6 0.0 collective-permute-start.4
  15.6 1.7 %near.1 = (f32[8,128]{1,0:T(8,128)S(1)}, f32[16,8,128]{2,1,0:T(8,128)S(1)}, bf16[8,32,256]{2,1,0:T(8,128)(2,1)S(1)}, bf16[156,3,16,128]{3,2,1,0:T(8,128)(2,1)S(1...) custom-call(f32[8,8,384]{2,1,0:T(8,128)S(1)} %constant_dynamic-update-slice_fusion.blocks_ref), custom_call_target="tpu_custom_call" | custom-call | flops 4000000000 | bytes 1048576 | tf_op jit(solution)/shard_map/near/pallas_call | solution.py:504
  17.3 0.6 %collective-permute-start.3 = (f32[8,128]{1,0:T(8,128)S(1)}, f32[8,128]{1,0:T(8,128)S(1)}, u32[]{:S(2)}, u32[]{:S(2)}) collective-permute-start(f32[8,128]{1,0:T(8,128)S(1)} %get-tuple-element.19.near_ref), channel_id=1, source_target_pairs={{0,2},{2,0},{4,6},{6,4},{8,10},{10,8},{12,14},{14,12},{1,3},{3,1},... | collective-permute-start | bytes 12296 | tf_op jit(solution)/shard_map/ppermute | solution.py:514
  17.8 0.0 collective-permute-done.4.blocks_ref
  17.8 3.0 %rest.1 = (f32[1,128]{1,0:T(1,128)S(1)}, f32[1,224]{1,0:T(1,128)S(1)}, f32[8,128]{1,0:T(8,128)S(1)}) custom-call(f32[8,8,384]{2,1,0:T(8,128)S(1)} %collective-permute-done.4.blocks_ref, s32[8,256]{1,0:T(8,128)S(1)} %get-tuple-element.20.rank_ref, f32[16,8,128]{2,1,0:T(8,128)S(1)} %get-tuple-element.21.src_ref, ...), custom_call_target="tpu_custom_call" | custom-call | flops 8000000000 | bytes 1048576 | tf_op jit(solution)/shard_map/rest/pallas_call | solution.py:517
  20.9 0.0 collective-permute-done.3.far_ref
  20.9 0.6 %finish.1 = (f32[1,128]{1,0:T(1,128)}, f32[1,224]{1,0:T(1,128)}, f32[1,1]{1,0:T(1,128)}) custom-call(f32[8,128]{1,0:T(8,128)S(1)} %get-tuple-element.19.near_ref, f32[8,128]{1,0:T(8,128)S(1)} %collective-permute-done.3.far_ref, f32[8,128]{1,0:T(8,128)S(1)} %get-tuple-element.27.cross_ref, f32[1,128]{1,0:T(1,128)S(1)} %get-tuple-element.28.frames_ref, ...), custom_call_target="tpu_custom_call" | custom-call | tf_op jit(solution)/shard_map/finish/pallas_call | solution.py:527
  (6 shorter events, 0.0 us)
Async XLA Ops:
  1.8 4.7 %collective-permute-start = (f32[1,8,384]{2,1,0:T(8,128)S(1)}, f32[1,8,384]{2,1,0:T(8,128)S(1)}, u32[]{:S(2)}, u32[]{:S(2)}) collective-permute-start(f32[1,8,384]{2,1,0:T(8,128)S(1)} %get-tuple-element.18), channel_id=1, source_target_pairs={{0,1},{1,0},{2,3},{3,2},{4,5},{5,4},{6,7},{7,6},{8,9},{9,8},{10,11... | collective-permute-start | bytes 36872 | tf_op jit(solution)/shard_map/ppermute | solution.py:487
  6.6 3.9 %collective-permute-start.1 = (f32[2,8,384]{2,1,0:T(8,128)S(1)}, f32[2,8,384]{2,1,0:T(8,128)S(1)}, u32[]{:S(2)}, u32[]{:S(2)}) collective-permute-start(f32[2,8,384]{2,1,0:T(8,128)S(1)} %pad_maximum_fusion.1), channel_id=1, source_target_pairs={{0,4},{2,6},{4,0},{6,2},{8,12},{10,14},{12,8},{14,10},{1,5},{3,7},... | collective-permute-start | bytes 73736 | tf_op jit(solution)/shard_map/ppermute | solution.py:487
  10.5 5.1 %collective-permute-start.2 = (f32[4,8,384]{2,1,0:T(8,128)S(1)}, f32[4,8,384]{2,1,0:T(8,128)S(1)}, u32[]{:S(2)}, u32[]{:S(2)}) collective-permute-start(f32[4,8,384]{2,1,0:T(8,128)S(1)} %pad_maximum_fusion), channel_id=1, source_target_pairs={{0,8},{2,10},{4,12},{6,14},{8,0},{10,2},{12,4},{14,6},{1,9},{3,11}... | collective-permute-start | bytes 147464 | tf_op jit(solution)/shard_map/ppermute | solution.py:487
  15.6 2.3 %collective-permute-start.4 = (f32[8,8,384]{2,1,0:T(8,128)S(1)}, f32[8,8,384]{2,1,0:T(8,128)S(1)}, u32[]{:S(2)}, u32[]{:S(2)}) collective-permute-start(f32[8,8,384]{2,1,0:T(8,128)S(1)} %constant_dynamic-update-slice_fusion.blocks_ref), channel_id=1, source_target_pairs={{0,2},{2,0},{4,6},{6,4},{8,10},{10,8},{12,14},{14,12},{1,3},{3,1},... | collective-permute-start | bytes 294920 | tf_op jit(solution)/shard_map/ppermute | solution.py:487
  17.3 3.6 %collective-permute-start.3 = (f32[8,128]{1,0:T(8,128)S(1)}, f32[8,128]{1,0:T(8,128)S(1)}, u32[]{:S(2)}, u32[]{:S(2)}) collective-permute-start(f32[8,128]{1,0:T(8,128)S(1)} %get-tuple-element.19.near_ref), channel_id=1, source_target_pairs={{0,2},{2,0},{4,6},{6,4},{8,10},{10,8},{12,14},{14,12},{1,3},{3,1},... | collective-permute-start | bytes 12296 | tf_op jit(solution)/shard_map/ppermute | solution.py:514
